TPU v7x, 128 devices: a whole 4x4x4 slice. The times are simulated.
128 devices in a mesh: rep: 2 (over core), dp: 64 (over x, y, z).
Axes of the slice: x: 4, y: 4, z: 4, core: 2. Of those that a mesh axis runs over, the one named last changes fastest.
Arguments:
- g_w_gate: bfloat16 [128, 2, 768, 1792], P(('rep', 'dp')), parts along dimension 0
- g_w_up: bfloat16 [128, 2, 768, 1792], P(('rep', 'dp')), parts along dimension 0
- g_w_down: bfloat16 [128, 2, 1792, 768], P(('rep', 'dp')), parts along dimension 0
- w_gate: bfloat16 [2, 768, 1792], replicated
- w_up: bfloat16 [2, 768, 1792], replicated
- w_down: bfloat16 [2, 1792, 768], replicated
- m_w_gate: float32 [2, 768, 1792], P(None, 'dp')
- m_w_up: float32 [2, 768, 1792], P(None, 'dp')
- m_w_down: float32 [2, 1792, 768], P(None, 'dp')
- v_w_gate: float32 [2, 768, 1792], P(None, 'dp')
- v_w_up: float32 [2, 768, 1792], P(None, 'dp')
- v_w_down: float32 [2, 1792, 768], P(None, 'dp')
Outputs:
- output 1: bfloat16 [4, 768, 1792], P('rep'), parts along dimension 0
- output 2: bfloat16 [4, 768, 1792], P('rep'), parts along dimension 0
- output 3: bfloat16 [4, 1792, 768], P('rep'), parts along dimension 0
- output 4: float32 [4, 768, 1792], P('rep', 'dp'), parts along dimension 0
- output 5: float32 [4, 768, 1792], P('rep', 'dp'), parts along dimension 0
- output 6: float32 [4, 1792, 768], P('rep', 'dp'), parts along dimension 0
- output 7: float32 [4, 768, 1792], P('rep', 'dp'), parts along dimension 0
- output 8: float32 [4, 768, 1792], P('rep', 'dp'), parts along dimension 0
- output 9: float32 [4, 1792, 768], P('rep', 'dp'), parts along dimension 0
There are 2 independent parts. A program takes and returns all parts, laid end to end along the dimension named above; an argument that names none is the same for every part.
All inputs are finite; a program needn't handle non-finite values.
Results may differ from a plain program's by a relative error of at most 0.022.
Values are sent between devices in bfloat16 or wider.
A program may use at most 1.5 GiB of HBM per device.

v0:
```python
import jax
import jax.numpy as jnp
from jax import lax
from jax.sharding import PartitionSpec as P


def adamw(w, m, v, g):
    m = 0.9 * m + 0.1 * g
    v = 0.95 * v + 0.05 * g * g
    step = m * lax.rsqrt(v + 1e-8) + 0.1 * w
    return (w - 0.02 * step).astype(jnp.bfloat16), m, v


def clipped(gradients, sum_of_squares, count):
    factor = jnp.minimum(1.0, 0.5 * lax.rsqrt(sum_of_squares / count + 1e-30))
    return [g * factor for g in gradients]


def solution(mesh):
    def step(*arrays):
        terms, weights, m, v = (arrays[i : i + 3] for i in (0, 3, 6, 9))
        gradients = [lax.psum_scatter(t[0], "dp", scatter_dimension=1, tiled=True).astype(jnp.float32) for t in terms]
        squares = lax.psum(sum(jnp.sum(g * g) for g in gradients), "dp")
        gradients = clipped(gradients, squares, lax.psum(1, "dp") * sum(g.size for g in gradients))
        me = lax.axis_index("dp")
        own = [lax.dynamic_slice_in_dim(w, me * one.shape[1], one.shape[1], 1).astype(jnp.float32) for w, one in zip(weights, m, strict=True)]
        new = [adamw(w, m, v, g) for w, m, v, g in zip(own, m, v, gradients, strict=True)]
        whole = [lax.all_gather(one[0], "dp", axis=1, tiled=True) for one in new]
        return (*whole, *(one[1] for one in new), *(one[2] for one in new))

    all_of, cut = P(None, None, None), P(None, "dp", None)
    return jax.shard_map(
        step,
        mesh=mesh,
        in_specs=(P(("rep", "dp"), None, None, None),) * 3 + (all_of,) * 3 + (cut,) * 6,
        out_specs=(P("rep", None, None),) * 3 + (P("rep", "dp", None),) * 6,
        check_vma=False,
    )
```

profile of v0, /device:TPU:0, one launch (start us, length us, event | category | flops | bytes accessed | tf_op | source)
XLA Modules:
  0.0 688.4 jit_solution(14488153618980011656)
XLA Ops:
  7.2 0.0 all-reduce.6.cloned.1.call-start
  7.2 0.0 copy-start
  7.2 0.0 slice-start
  7.2 25.7 %copy.48 = bf16[1,2,1792,768]{3,1,2,0:T(2,128)(2,1)} copy(bf16[1,2,1792,768]{3,2,1,0:T(8,128)(2,1)} %param.14) | data formatting | bytes 11010048 | tf_op args[2]
  32.9 0.0 copy-done
  32.9 0.0 slice-start.1
  33.0 17.1 %copy.49 = bf16[1,2,768,1792]{3,1,2,0:T(2,128)(2,1)} copy(bf16[1,2,768,1792]{3,2,1,0:T(8,128)(2,1)S(1)} %copy-done) | data formatting | bytes 11010048 | tf_op args[1]
  50.0 0.0 slice-done
  50.0 0.0 slice-done.1
  50.0 17.1 %copy.50 = bf16[1,2,768,1792]{3,1,2,0:T(2,128)(2,1)} copy(bf16[1,2,768,1792]{3,2,1,0:T(8,128)(2,1)S(1)} %bitcast.14) | data formatting | bytes 11010048 | tf_op args[0]
  67.1 0.0 copy-start.7
  67.1 0.0 copy-start.1
  67.1 0.0 copy-start.2
  67.1 0.0 copy-start.3
  67.1 0.0 copy-start.4
  67.1 0.0 copy-start.5
  67.1 0.0 copy-start.6
  67.1 0.0 all-reduce.6.cloned.1.call-update
  67.2 0.0 all-gather.6.cloned.1.call-start
  67.2 0.5 copy-done.7
  67.7 0.6 dynamic-slice
  69.6 214.0 %all-reduce.6.cloned.1.call-done = (bf16[2,768,1792]{2,0,1:T(2,128)(2,1)}, bf16[2,768,1792]{2,0,1:T(2,128)(2,1)}, bf16[2,1792,768]{2,0,1:T(2,128)(2,1)}) async-done(((bf16[2,768,1792]{2,0,1:T(2,128)(2,1)}, bf16[2,768,1792]{2,0,1:T(2,128)(2,1)}, bf16[2,1792,768]{2,0,1:T(2,128)(2,1)}), (bf16[2,768,1792]{2,0,1:T(2,128)(2,1)}, bf16[2,768,1792]{2,0,1:T(2,128)(2,1)}, ...) | async-done | bytes 16515088
  283.6 1.7 fusion.8
  286.6 1.7 fusion.10
  289.0 1.1 constant_dynamic-slice_fusion.1
  290.1 176.5 %psum.7 = f32[]{:T(128)} all-reduce(f32[]{:T(128)S(6)} %add.65), channel_id=1, replica_groups=mesh['rep'=2,'dp'=64] {'dp'}, use_global_device_ids=true, to_apply=%region_6.0 | all-reduce | flops 1 | bytes 8 | tf_op jit(solution)/shard_map/psum | solution.py:23
  467.3 0.0 copy-done.1
  467.3 0.0 copy-done.2
  467.3 2.1 fusion.19
  469.4 0.0 all-gather.6.cloned.1.call-update
  469.4 0.0 all-gather.4.cloned.1.call-start
  469.4 0.0 copy-done.3
  469.4 0.0 copy-done.4
  469.5 2.1 fusion.18
  471.5 0.0 all-gather.4.cloned.1.call-update
  471.5 0.0 all-gather.8.cloned.1.call-start
  471.6 0.9 constant_dynamic-slice_fusion
  472.5 0.0 copy-done.5
  472.6 0.0 copy-done.6
  472.6 2.1 fusion.20
  474.7 0.0 all-gather.8.cloned.1.call-update
  474.7 58.4 %all-gather.6.cloned.1.call-done = bf16[2,768,1792]{2,0,1:T(2,128)(2,1)} async-done(((bf16[2,12,1792]{2,0,1:T(2,128)(2,1)}), bf16[2,768,1792]{2,0,1:T(2,128)(2,1)}) %all-gather.6.cloned.1.call-update) | async-done | bytes 5505040 | tf_op jit(solution)/shard_map/all_gather | solution.py:28
  533.0 5.7 copy.37
  538.7 66.2 %all-gather.4.cloned.1.call-done = bf16[2,768,1792]{2,0,1:T(2,128)(2,1)} async-done(((bf16[2,12,1792]{2,0,1:T(2,128)(2,1)}), bf16[2,768,1792]{2,0,1:T(2,128)(2,1)}) %all-gather.4.cloned.1.call-update) | async-done | bytes 5505040 | tf_op jit(solution)/shard_map/all_gather | solution.py:28
  605.0 5.7 copy.36
  610.7 65.5 %all-gather.8.cloned.1.call-done = bf16[2,1792,768]{2,0,1:T(2,128)(2,1)} async-done(((bf16[2,28,768]{2,0,1:T(2,128)(2,1)}), bf16[2,1792,768]{2,0,1:T(2,128)(2,1)}) %all-gather.8.cloned.1.call-update) | async-done | bytes 5505040 | tf_op jit(solution)/shard_map/all_gather | solution.py:28
  676.2 5.7 copy.38
  (1 shorter events, 0.0 us)
Async XLA Ops:
  7.2 276.4 %all-reduce.6.cloned.1.call-start = ((), (), s32[]{:S(2)}) async-start(), calls=%async_computation.3 | async-start | bytes 33030144
  7.2 25.7 %copy-start = (bf16[1,2,768,1792]{3,2,1,0:T(8,128)(2,1)S(1)}, bf16[1,2,768,1792]{3,2,1,0:T(8,128)(2,1)}, u32[]{:S(2)}) copy-start(bf16[1,2,768,1792]{3,2,1,0:T(8,128)(2,1)} %param.13) | copy-start | bytes 16515076
  7.2 42.8 %slice-start = ((s8[5505024]{0:T(1024)(128)(4,1)}), s8[4194304]{0:T(1024)(128)(4,1)S(1)}, s32[]{:S(2)}) async-start(s8[5505024]{0:T(1024)(128)(4,1)} %bitcast.13), calls=%async_computation.4 | async-start | bytes 8388608
  32.9 17.1 %slice-start.1 = ((s8[5505024]{0:T(1024)(128)(4,1)}), s8[1310720]{0:T(1024)(128)(4,1)S(1)}, s32[]{:S(2)}) async-start(s8[5505024]{0:T(1024)(128)(4,1)} %bitcast.13), calls=%async_computation.5 | async-start | bytes 2621440
  67.1 0.7 copy-start.7
  67.1 400.2 %copy-start.1 = (f32[2,12,1792]{2,0,1:T(2,128)S(1)}, f32[2,12,1792]{2,0,1:T(2,128)}, u32[]{:S(2)}) copy-start(f32[2,12,1792]{2,0,1:T(2,128)} %param.22) | copy-start | bytes 516100
  67.1 400.2 %copy-start.2 = (f32[2,12,1792]{2,0,1:T(2,128)S(1)}, f32[2,12,1792]{2,0,1:T(2,128)}, u32[]{:S(2)}) copy-start(f32[2,12,1792]{2,0,1:T(2,128)} %param.19) | copy-start | bytes 516100
  67.1 402.3 %copy-start.3 = (f32[2,12,1792]{2,0,1:T(2,128)S(1)}, f32[2,12,1792]{2,0,1:T(2,128)}, u32[]{:S(2)}) copy-start(f32[2,12,1792]{2,0,1:T(2,128)} %param.21) | copy-start | bytes 516100
  67.1 402.3 %copy-start.4 = (f32[2,12,1792]{2,0,1:T(2,128)S(1)}, f32[2,12,1792]{2,0,1:T(2,128)}, u32[]{:S(2)}) copy-start(f32[2,12,1792]{2,0,1:T(2,128)} %param.18) | copy-start | bytes 516100
  67.1 405.4 %copy-start.5 = (f32[2,28,768]{2,0,1:T(2,128)S(1)}, f32[2,28,768]{2,0,1:T(2,128)}, u32[]{:S(2)}) copy-start(f32[2,28,768]{2,0,1:T(2,128)} %param.23) | copy-start | bytes 516100
  67.1 405.4 %copy-start.6 = (f32[2,28,768]{2,0,1:T(2,128)S(1)}, f32[2,28,768]{2,0,1:T(2,128)}, u32[]{:S(2)}) copy-start(f32[2,28,768]{2,0,1:T(2,128)} %param.20) | copy-start | bytes 516100
  67.2 465.9 %all-gather.6.cloned.1.call-start = ((), (), s32[]{:S(2)}) async-start(), calls=%async_computation.1 | async-start | bytes 5591040 | tf_op jit(solution)/shard_map/all_gather | solution.py:28
  469.4 135.6 %all-gather.4.cloned.1.call-start = ((), (), s32[]{:S(2)}) async-start(), calls=%async_computation | async-start | bytes 5591040 | tf_op jit(solution)/shard_map/all_gather | solution.py:28
  471.5 204.6 %all-gather.8.cloned.1.call-start = ((), (), s32[]{:S(2)}) async-start(), calls=%async_computation.2 | async-start | bytes 5591040 | tf_op jit(solution)/shard_map/all_gather | solution.py:28
Sparse Core Ops, SparseCore 0:
  67.3 216.2 all-reduce.5
  469.5 63.4 all-gather.5
  536.5 68.4 all-gather.3
  607.7 68.4 all-gather.7
where the time goes:
time: 689 us; the launch traced here: 688 us
  waiting for transfers between devices  404 us (59%)
  blocking collectives  177 us (26%)
  local copies, waits for them, and re-layouts  80.1 us (12%)
  between operations  17.9 us (3%)
  other arithmetic  9.63 us (1%)
    unnamed x5, waiting for transfers between devices  214 us
    all_gather x3, waiting for transfers between devices, step(): whole = [lax.all_gather(one[0], 'dp', axis=1, tiled=True) for one in new]  190 us
    psum x1, blocking collectives, step(): squares = lax.psum(sum((jnp.sum(g * g) for g in gradients)), 'dp')  177 us
    unnamed x27, local copies, waits for them, and re-layouts  78 us
  transfers between devices with their start and end apart: 4, of which 4 were waited for; matrix products, arithmetic and copies ran while one was open for 2% of the time, Pallas kernels for 0%

commit v1 on v0

v1 whole, which is shorter than its diff:
```python
import jax
import jax.numpy as jnp
from jax import lax
from jax.experimental import pallas as pl
from jax.experimental.pallas import tpu as pltpu
from jax.sharding import PartitionSpec as P

UP, DOWN, GATE = WEIGHTS = range(3)
N = 4
QUARTERS = range(N)
FLOWS = BOTH = range(2)
ALL = [(w, h) for h in FLOWS for w in WEIGHTS]
STRIDE = {"x": N * N, "y": N, "z": 1}
AXES = (("x", "y", "z"), ("y", "z", "x"), ("z", "x", "y"))
CHUNK_AXIS = ("y", "x", "x")
FAR_FIRST = (2, 1, 3)
OUTWARD = (0, -1, 1, 2)
NEAR = (-1, 1)
TILE = 16
BF, F32 = jnp.bfloat16, jnp.float32


def fori(n, body):
    lax.fori_loop(0, n, lambda i, c: (body(i), c)[1], 0)


def main_kernel(names, count, *refs):
    R = dict(zip(names, refs, strict=True))

    def three(name):
        return [R[name, w] for w in WEIGHTS]

    g, wt, mi, vi, W, mo, vo = (three(n) for n in ("g", "wt", "mi", "vi", "W", "mo", "vo"))
    own1, own2, r, ws, ms, vs, pieces = (three(n) for n in ("own1", "own2", "r", "ws", "ms", "vs", "pieces"))
    wl, mv = ([R[n, UP], R[n, DOWN], R[n, UP]] for n in ("wl", "mv"))
    tall = [R["tall", UP], R["tall", DOWN], R["tall", UP]]
    qa = {w: R["qa", w] for w in (UP, GATE)}
    gf = mo
    pb, bs, qb, bt, rb, fa, sa, ra, fc, sc, rc, tsc, tc, ub, uc, vc, nsend, nrecv = (
        R[n] for n in ("pb", "bs", "qb", "bt", "rb", "fa", "sa", "ra", "fc", "sc", "rc", "tsc", "tc", "ub", "uc", "vc", "nsend", "nrecv")
    )
    ua = sa
    sent, local, rec1, rec2, rec2b, rec3, recn, rech, recy, reco = (
        R[n] for n in ("sent", "local", "rec1", "rec2", "rec2b", "rec3", "recn", "rech", "recy", "reco")
    )
    tokens = iter(range(sent.shape[0]))
    leaving = []

    me = lax.axis_index("dp")
    co = {"x": me // STRIDE["x"], "y": me // STRIDE["y"] % N, "z": me % N}
    x, y, z = co["x"], co["y"], co["z"]

    def at(axis, off):
        return (co[axis] + off) % N

    def to(axis, off):
        return me + (at(axis, off) - co[axis]) * STRIDE[axis]

    def group(ref):
        sem = sent.at[next(tokens)]
        leaving.append((ref, sem))
        return sem

    def post(src, dst, ssem, rsem, device):
        pltpu.make_async_remote_copy(
            src_ref=src, dst_ref=dst, send_sem=ssem, recv_sem=rsem, device_id={"dp": device}, device_id_type=pl.DeviceIdType.MESH
        ).start()

    def send(src, dst, ssem, rsem, axis, off):
        post(src, dst, ssem, rsem, to(axis, off))

    def wait(ref, sem):
        pltpu.make_async_copy(ref, ref, sem).wait()

    def way(h):
        return 1 - 2 * h

    def offs(w, h):
        return (2, 1, -1, 0) if w == DOWN else (2, -way(h), way(h), 0)

    def term(w, h, q, c):
        if w == UP:
            return g[w].at[h, q, c]
        if w == DOWN:
            return g[w].at[h, c, q]
        cols = g[w].shape[-1] // 2
        return g[w].at[q // 2, c, h, :, pl.ds(pl.multiple_of(q % 2 * cols, 128), cols)]

    def tiles(n, body):
        fori(n // TILE, lambda i: body(pl.ds(pl.multiple_of(i * TILE, TILE), TILE)))

    def cut(w):
        rows, (_, pad, cols) = vi[w].shape[0], pieces[w].shape
        for q in QUARTERS:
            pieces[w][q] = tall[w][rows * q : rows * q + pad, 0:cols]

    def join(w, piece, cols):
        rows = vi[w].shape[0]
        for q in QUARTERS:
            tall[w][rows * q : rows * q + rows, 0:cols] = piece(q).astype(F32)[:rows]
        return tall[w][0 : N * rows, 0:cols].astype(BF)

    barrier = pltpu.get_barrier_semaphore()
    for axis in STRIDE:
        for off in FAR_FIRST:
            pl.semaphore_signal(barrier, inc=1, device_id={"dp": to(axis, off)}, device_id_type=pl.DeviceIdType.MESH)

    for which, buf in enumerate((own1, own2)):
        for w, h in ALL:
            q = at(AXES[w][0], way(h) * (1 - which))
            for k in QUARTERS:
                src = term(w, h, q, at(CHUNK_AXIS[w], offs(w, h)[k]))
                pltpu.make_async_copy(src, buf[w].at[h, k], local.at[which, w, h]).start()
    pl.semaphore_wait(barrier, len(STRIDE) * len(FAR_FIRST))

    left1 = [group(r[w]) for w in WEIGHTS]

    def phase1(i, w, h, k, src, off):
        send(src, r[w].at[i, h, k], left1[w], rec1.at[w, i, h, k], AXES[w][0], off)

    for i, (far, near) in enumerate(((2, 1), (-1, -1))):
        for k in QUARTERS:
            for w, h in ALL:
                s = way(h)
                src = term(w, h, at(AXES[w][0], far * s), at(CHUNK_AXIS[w], offs(w, h)[k]))
                phase1(i, w, h, k, src, near * s)

    def load_state(w):
        for i, (src, dst) in enumerate(((wt[w].at[:, x, y], wl[w]), (mi[w], mv[w].at[0]), (vi[w], mv[w].at[1]))):
            pltpu.make_async_copy(src, dst, local.at[2 + i // 2, w, i % 2]).start()

    load_state(UP)
    load_state(DOWN)
    for which, buf in enumerate((own1, own2)):
        for w, h in ALL:
            wait(buf[w].at[h], local.at[which, w, h])

    for k in QUARTERS:
        for w, h in ALL:
            wait(r[w].at[0, h, k], rec1.at[w, 0, h, k])

            def add(t, w=w, h=h, k=k):
                own1[w][h, k, t] = (own1[w][h, k, t].astype(F32) + r[w][0, h, k, t].astype(F32)).astype(BF)

            tiles(own1[w].shape[2], add)
            phase1(2, w, h, k, own1[w].at[h, k], way(h))

    for w in WEIGHTS:
        rows, (_, pad, cols) = vi[w].shape[0], ms[w].shape
        if w != GATE:
            n = N * rows
            tall[w][n : n + TILE, :] = jnp.zeros((TILE, tall[w].shape[1]), F32)
        for i, dst in enumerate((wl[w], mv[w].at[0], mv[w].at[1])):
            wait(dst, local.at[2 + i // 2, w, i % 2])
        for h in BOTH:
            for dst in (ms[w], vs[w]):
                dst[h, pad - 8 : pad] = jnp.zeros((8, cols), F32)

        def spread(i, w=w):
            for src, dst in ((mv[w][0, i], ms[w]), (mv[w][1, i], vs[w])):
                for h in BOTH:
                    dst[h, pl.ds(i, 1), :] = src[h : h + 1]

        fori(rows, spread)
        for h in BOTH:

            def widen(t, w=w, h=h):
                tall[w][t, :] = wl[w][h, t].astype(F32)

            tiles(N * rows, widen)
            src = pieces[w] if w != GATE else pieces[UP]
            cut(w if w != GATE else UP)
            ws[w][h] = src[z]
        if w == UP:
            load_state(GATE)

    def total(w, h, k, t):
        return own2[w][h, k, t].astype(F32) + r[w][1, h, k, t].astype(F32) + r[w][2, h, k, t].astype(F32)

    def cut_down(h, k):
        def put(t):
            tall[DOWN][t, :] = total(DOWN, h, k, t)

        tiles(own2[DOWN].shape[2], put)
        cut(DOWN)

    left2 = {w: group(qa[w]) for w in qa}
    left2b = group(qb)

    def phase2(i, w, h, off):
        send(own2[w].at[h, i], qa[w].at[h, i], left2[w], rec2.at[w // 2, h, i], AXES[w][1], off)

    def phase2b(i, h, k, off):
        send(bs.at[h, k, i], qb.at[h, k, i], left2b, rec2b.at[h, k, i], "z", off)

    for k in QUARTERS:
        for w, h in ALL:
            s = way(h)
            for i in (1, 2):
                wait(r[w].at[i, h, k], rec1.at[w, i, h, k])
            if w == DOWN:
                cut_down(h, k)
                pb[h, k] = pieces[w][z]
                for i, (far, near) in enumerate(((2, 1), (-1, -1))):
                    bs[h, k, i] = pieces[w][at("z", far * s)].astype(BF)
                    phase2b(i, h, k, near * s)
            elif k < 2:

                def put(t, w=w, h=h, k=k):
                    own2[w][h, k, t] = total(w, h, k, t).astype(BF)

                tiles(own2[w].shape[2], put)
                phase2(k, w, h, -s if k else s)

    for w, h in ALL:
        s = way(h)
        if w == DOWN:
            for k in QUARTERS:
                cut_down(h, k)
                wait(qb.at[h, k, 0], rec2b.at[h, k, 0])
                bs[h, k, 2] = (pieces[w][at("z", s)] + qb[h, k, 0].astype(F32)).astype(BF)
                phase2b(2, h, k, s)
        else:
            wait(qa[w].at[h, 0], rec2.at[w // 2, h, 0])

            def add2(t, w=w, h=h):
                own2[w][h, 2, t] = (total(w, h, 2, t) + qa[w][h, 0, t].astype(F32)).astype(BF)

            tiles(own2[w].shape[2], add2)
            phase2(2, w, h, s)

    left_a, left_c, left_b = group(ra), group(rc), group(rb)
    for w in qa:
        for h in BOTH:
            for i in (1, 2):
                wait(qa[w].at[h, i], rec2.at[w // 2, h, i])

            def total2(t, w=w, h=h):
                return total(w, h, 3, t) + qa[w][h, 1, t].astype(F32) + qa[w][h, 2, t].astype(F32)

            if w == UP:

                def put2(t, total2=total2):
                    tall[UP][t, :] = total2(t)

                tiles(own2[w].shape[2], put2)
                cut(UP)
                for q in QUARTERS:
                    sa[q, h] = pieces[UP][q].astype(BF)
                fa[h] = pieces[UP][z]
            else:
                n = fc.shape[1]
                for b in BOTH:

                    def put2(i, total2=total2, h=h, b=b, n=n):
                        v = total2(pl.ds(pl.multiple_of(b * n + i * TILE, TILE), TILE))
                        t = pl.ds(pl.multiple_of(i * TILE, TILE), TILE)
                        fc[2 * h + b, t] = v
                        sc[2 * h + b, t] = v.astype(BF)

                    fori(n // TILE, put2)
        for j in FAR_FIRST:
            if w == UP:
                send(sa.at[at("z", j)], ra.at[j - 1], left_a, rec3.at[0, j - 1], "z", j)
            else:
                send(sc.at[at("y", j)], rc.at[j - 1], left_c, rec3.at[1, j - 1], "y", j)
    for k in QUARTERS:
        for h in BOTH:
            for i in (1, 2):
                wait(qb.at[h, k, i], rec2b.at[h, k, i])
            v = pb[h, k] + qb[h, k, 1].astype(F32) + qb[h, k, 2].astype(F32)
            off = offs(DOWN, h)[k]
            if off:
                bt[h, k] = v.astype(BF)
                send(bt.at[h, k], rb.at[h, k], left_b, rec3.at[2 + h, k], "x", off)
            else:
                pb[h, k] = v

    def fold(v):
        v = jnp.sum(v * v, axis=0, keepdims=True)
        out = v[:, 0:128]
        for i in range(128, v.shape[1], 128):
            out = out + v[:, i : i + 128]
        nsend[...] = nsend[...] + out

    def valid(n, v):
        return jnp.where(lax.broadcasted_iota(jnp.int32, v.shape, 0) < n, v, 0.0)

    def rounded(own, others):
        for o in others:
            own = own + o.astype(F32)
        return own.astype(BF).astype(F32)

    others = range(len(FAR_FIRST))
    half = tsc.shape[-1]
    nsend[...] = jnp.zeros(nsend.shape, F32)
    for j in others:
        wait(rc.at[j], rec3.at[1, j])

    def last_c(t):
        v = rounded(fc[y, t], [rc[j, t] for j in others])
        tall[UP][t, 0:half] = v
        fold(v)

    tiles(fc.shape[1], last_c)
    cut(GATE)
    for q in QUARTERS:
        tsc[q] = pieces[GATE][q].astype(BF)
    tc[z] = tsc[z]
    left = group(tc.at[0:3])
    for j in FAR_FIRST:
        send(tsc.at[at("z", j)], tc.at[z], left, rech.at[0, j - 1], "z", j)
    for j in others:
        wait(ra.at[j], rec3.at[0, j])
    (gone,) = [i for i, (_, sem) in enumerate(leaving) if sem is left_a]
    wait(*leaving.pop(gone))
    for h in BOTH:
        v = rounded(fa[h], [ra[j, h] for j in others])
        gf[UP][h] = v
        fold(valid(vi[UP].shape[0], v))
    for h in BOTH:
        for k in others:
            wait(rb.at[h, k], rec3.at[2 + h, k])
        v = rounded(pb[h, 3], [rb[h, k] for k in others])
        gf[DOWN][h] = v
        fold(valid(vi[DOWN].shape[0], v))

    devices = nrecv.shape[0]
    nrecv[me] = nsend[...]
    left = group(nrecv.at[1:devices])
    fori(devices - 1, lambda i: post(nsend, nrecv.at[me], left, recn.at[0], (me + 1 + i) % devices))
    for j in FAR_FIRST:
        wait(tc.at[at("z", -j)], rech.at[0, j - 1])
    wait(nrecv.at[1:devices], recn.at[0])
    squares = jnp.sum(jnp.sum(nrecv[...], axis=0), axis=1, keepdims=True)
    factor = jnp.minimum(1.0, 0.5 * lax.rsqrt(squares / count + 1e-30))
    for q in QUARTERS:
        gf[GATE][q // 2, :, half * (q % 2) : half * (q % 2 + 1)] = tc[q].astype(F32)

    def adamw(w, h):
        gc = gf[w][h] * factor
        m = 0.9 * ms[w][h] + 0.1 * gc
        v = 0.95 * vs[w][h] + 0.05 * gc * gc
        mo[w][h] = m
        vo[w][h] = v
        step = m * lax.rsqrt(v + 1e-8) + 0.1 * ws[w][h]
        return (ws[w][h] - 0.02 * step).astype(BF)

    def spread_out(i, axis, ref, src, first):
        left = group(first)
        for j in FAR_FIRST:
            send(src(at(axis, j)), ref(co[axis]), left, rech.at[i, j - 1], axis, j)

    def arrived(i, axis, ref):
        for j in FAR_FIRST:
            wait(ref(at(axis, -j)), rech.at[i, j - 1])

    for h in BOTH:
        new = adamw(GATE, h)
        vc[2 * h] = new[:, :half]
        vc[2 * h + 1] = new[:, half:]
    uc[z] = vc[z]
    spread_out(1, "z", lambda p: uc.at[p], lambda p: vc.at[p], uc.at[0:3])
    for h in BOTH:
        ua[z, h] = adamw(UP, h)
    spread_out(2, "z", lambda p: ua.at[p], lambda p: ua.at[z], ua.at[0:3])
    for h in BOTH:
        ub[z, x, h] = adamw(DOWN, h)
    spread_out(3, "x", lambda p: ub.at[z, p], lambda p: ub.at[z, x], ub.at[0, 0:3])

    def own_out(block, left, recv, axis):
        for d in BOTH:
            ref = block(0, None)
            send(ref, ref, left, recv.at[0, d], axis, way(d))

    def pass_on(block, left, recv, axis):
        for d in BOTH:
            wait(block(NEAR[d], None), recv.at[0, d])
            ref = block(NEAR[d], d)
            send(ref, ref, left, recv.at[1, d], axis, way(d))

    def passed(block, recv):
        for d in BOTH:
            wait(block(2, d), recv.at[1, d])

    def ring(ref, sub):
        def block(p, d):
            one = ref(p)
            return one if d is None else one.at[sub(d)]

        return block

    def one(d):
        return d

    def two(d):
        return pl.ds(2 * d, 2)

    left_o = [group(W[w].at[0:3]) for w in WEIGHTS]

    def outer(w, i):
        return ring(lambda p: W[w].at[at(AXES[w][0], p), at(CHUNK_AXIS[w], OUTWARD[i])], two if w == GATE else one)

    def outer_start(w, i):
        own_out(outer(w, i), left_o[w], reco.at[w, i], AXES[w][0])

    left_z, left_y, left_x = group(ub.at[0:3]), group(W[UP].at[0, 0:3]), group(W[GATE].at[0, 0:3])
    zring = [ring(lambda p, off=off: ub.at[at("z", p), at("x", off)], one) for off in OUTWARD]
    own_out(zring[0], left_z, recy.at[2], "z")

    arrived(1, "z", lambda p: uc.at[p])
    W[GATE][z, x, y] = join(GATE, lambda q: uc[q], half)
    spread_out(4, "y", lambda p: W[GATE].at[z, x, p], lambda p: W[GATE].at[z, x, y], W[GATE].at[0, 0, 0:3])

    arrived(2, "z", lambda p: ua.at[p])
    for h in BOTH:
        W[UP][x, y, h] = join(UP, lambda q: ua[q, h], tall[UP].shape[1])
    yring = ring(lambda p: W[UP].at[x, at("y", p)], one)
    own_out(yring, left_y, recy.at[0], "y")
    outer_start(UP, 0)

    for i, off in enumerate(OUTWARD):
        if off:
            wait(ub.at[z, at("x", off)], rech.at[3, -off % N - 1])
            own_out(zring[i], left_z, recy.at[2 + i], "z")
    for i in QUARTERS:
        pass_on(zring[i], left_z, recy.at[2 + i], "z")

    arrived(4, "y", lambda p: W[GATE].at[z, x, p])
    xring = ring(lambda p: W[GATE].at[z, at("x", p)], two)
    own_out(xring, left_x, recy.at[1], "x")
    outer_start(GATE, 0)

    pass_on(yring, left_y, recy.at[0], "y")
    outer_start(UP, 1)
    outer_start(UP, 2)
    for i in QUARTERS:
        passed(zring[i], recy.at[2 + i])
        c = at("x", OUTWARD[i])
        for h in BOTH:
            W[DOWN][y, c, h] = join(DOWN, lambda q: ub[q, c, h], tall[DOWN].shape[1])
        outer_start(DOWN, i)
    pass_on(xring, left_x, recy.at[1], "x")
    outer_start(GATE, 1)
    outer_start(GATE, 2)
    passed(yring, recy.at[0])
    outer_start(UP, 3)
    passed(xring, recy.at[1])
    outer_start(GATE, 3)
    for i in QUARTERS:
        for w in WEIGHTS:
            pass_on(outer(w, i), left_o[w], reco.at[w, i], AXES[w][0])
    for i in QUARTERS:
        for w in WEIGHTS:
            passed(outer(w, i), reco.at[w, i])
    for ref, sem in leaving:
        wait(ref, sem)


def write_kernel(names, *refs):
    R = dict(zip(names, refs, strict=True))
    W = [R["W", w] for w in WEIGHTS]
    out = [R["out", w] for w in WEIGHTS]
    half = W[GATE].shape[-1]
    copies = []
    for p in QUARTERS:
        for h in BOTH:
            cols, two = pl.ds(half * (p % 2), half), pl.ds(2 * h, 2)
            pairs = (
                (W[UP].at[p, :, h], out[UP].at[h, p]),
                (W[DOWN].at[p, :, h], out[DOWN].at[h, :, p]),
                (W[GATE].at[p, two], out[GATE].at[p // 2, two, :, :, cols]),
            )
            copies += [pltpu.make_async_copy(*pair, R["sem"].at[w, p, h]) for w, pair in enumerate(pairs)]
    for c in copies:
        c.start()
    for w in WEIGHTS:

        def gather(i, w=w):
            for n in "mv":
                for h in BOTH:
                    R[n + "b", w][i, h : h + 1] = R[n + "o", w][h, pl.ds(i, 1), :]

        fori(R["mb", w].shape[0], gather)
        for i, n in enumerate("mv"):
            copies.append(pltpu.make_async_copy(R[n + "b", w], R[n + "out", w], R["small"].at[i, w]))
            copies[-1].start()
    for c in copies:
        c.wait()


def call(kernel, ins, outs, scratch, place_in, place_out, **params):
    names = (*ins, *outs, *scratch)
    got = pl.pallas_call(
        lambda *refs: kernel(names, *refs),
        out_shape=list(outs.values()),
        in_specs=[pl.BlockSpec(memory_space=place_in)] * len(ins),
        out_specs=[pl.BlockSpec(memory_space=place_out)] * len(outs),
        scratch_shapes=list(scratch.values()),
        name=kernel.__name__,
        compiler_params=pltpu.CompilerParams(**params),
    )(*ins.values())
    return dict(zip(outs, got, strict=True))


def by_weight(**of):
    return {(n, w): t for n, ts in of.items() for w, t in zip(WEIGHTS, ts)}


def solution(mesh):
    def step(*arrays):
        terms, weights, m, v = ([arrays[i + j] for j in (1, 2, 0)] for i in (0, 3, 6, 9))
        (rows, ff), (rows_d, d) = m[0].shape[1:], m[1].shape[1:]
        half, n, n_d = ff // 2, N * rows, N * rows_d
        full = ((2, N, N, n, ff), (2, N, N, n_d, d), (2, N, N, n, ff))
        g = [t.reshape(s) for t, s in zip(terms, (*full[:2], (2, N, 2, 2 * n, ff)))]
        state = [[pltpu.with_memory_space_constraint(a.transpose(1, 0, 2), pltpu.HBM) for a in t] for t in (m, v)]
        weights = [a.reshape(s) for a, s in zip(weights, full)]
        ins = by_weight(g=g, wt=weights, mi=state[0], vi=state[1])

        vm, dma = pltpu.VMEM, pltpu.SemaphoreType.DMA
        pad, pad_d = 16, 32
        chunk = ((n, ff), (n_d, d), (2 * n, half))
        own = ((2, pad, ff), (2, pad_d, d), (2, pad, ff))
        pieces = [vm((N, *s), F32) for s in ((pad, ff), (pad_d, d), (pad, half))]
        scratch = by_weight(
            own1=[vm((2, N, *c), BF) for c in chunk],
            own2=[vm((2, N, *c), BF) for c in chunk],
            r=[vm((3, 2, N, *c), BF) for c in chunk],
            ws=[vm(s, F32) for s in own],
            ms=[vm(s, F32) for s in own],
            vs=[vm(s, F32) for s in own],
            pieces=pieces,
            wl=[vm((2, *c), BF) for c in chunk[:2]],
            mv=[vm((2, *a.shape), F32) for a in state[0][:2]],
            tall=[vm((n + TILE, ff), F32), vm((n_d + TILE, d), F32)],
        )
        scratch |= {("qa", w): vm((2, 3, *chunk[w]), BF) for w in (UP, GATE)}
        scratch |= dict(
            pb=vm((2, N, pad_d, d), F32),
            bs=vm((2, N, 3, pad_d, d), BF),
            qb=vm((2, N, 3, pad_d, d), BF),
            bt=vm((2, 3, pad_d, d), BF),
            rb=vm((2, 3, pad_d, d), BF),
            fa=vm((2, pad, ff), F32),
            sa=vm((N, 2, pad, ff), BF),
            ra=vm((3, 2, pad, ff), BF),
            fc=vm((N, n, half), F32),
            sc=vm((N, n, half), BF),
            rc=vm((3, n, half), BF),
            tsc=vm((N, pad, half), BF),
            tc=vm((N, pad, half), BF),
            ub=vm((N, N, 2, pad_d, d), BF),
            uc=vm((N, pad, half), BF),
            vc=vm((N, pad, half), BF),
            nsend=vm((1, 128), F32),
            nrecv=vm((N**3, 1, 128), F32),
            sent=dma((24,)),
            local=dma((N, 3, 2)),
            rec1=dma((3, 3, 2, N)),
            rec2=dma((2, 2, 3)),
            rec2b=dma((2, N, 3)),
            rec3=dma((N, 3)),
            recn=dma((1,)),
            rech=dma((5, 3)),
            recy=dma((6, 2, 2)),
            reco=dma((3, N, 2, 2)),
        )
        outs = by_weight(
            W=[jax.ShapeDtypeStruct(s, BF) for s in ((N, N, 2, n, ff), (N, N, 2, n_d, d), (N, N, N, n, half))],
            mo=[jax.ShapeDtypeStruct(s, F32) for s in own],
            vo=[jax.ShapeDtypeStruct(s, F32) for s in own],
        )
        count = float(N**3 * sum(a.size for a in m))

        def main(names, *refs):
            main_kernel(names, count, *refs)

        got = call(main, ins, outs, scratch, pltpu.HBM, vm, collective_id=0, has_side_effects=True, vmem_limit_bytes=36900000)
        small = [jax.ShapeDtypeStruct(a.shape, F32) for a in state[0]]
        outs = by_weight(out=[jax.ShapeDtypeStruct(s, BF) for s in full], mout=small, vout=small)
        scratch = by_weight(mb=[vm(a.shape, F32) for a in small], vb=[vm(a.shape, F32) for a in small])
        scratch |= dict(sem=dma((3, N, 2)), small=dma((2, 3)))
        new = call(write_kernel, got, outs, scratch, vm, pltpu.HBM, vmem_limit_bytes=2000000)
        back = (GATE, UP, DOWN)
        whole = [new["out", w].reshape(2, -1, full[w][-1]) for w in back]
        return (*whole, *(new[n, w].transpose(1, 0, 2) for n in ("mout", "vout") for w in back))

    all_of, part = P(None, None, None), P(None, "dp", None)
    return jax.shard_map(
        step,
        mesh=mesh,
        in_specs=(P(("rep", "dp"), None, None, None),) * 3 + (all_of,) * 3 + (part,) * 6,
        out_specs=(P("rep", None, None),) * 3 + (P("rep", "dp", None),) * 6,
        check_vma=False,
    )
```

time: 689 us -> 154 us (0.22)
  waiting for transfers between devices: 404 us -> 0 us
  blocking collectives: 177 us -> 0 us
  Pallas kernels: 0 us -> 153 us
  local copies, waits for them, and re-layouts: 80.1 us -> 0 us
  between operations: 17.9 us -> 0.65 us
  other arithmetic: 9.63 us -> 0 us
    unnamed x5 -> x0, waiting for transfers between devices: 214 us -> none
    all_gather x3 -> x0, waiting for transfers between devices: 190 us -> none  [step(): whole = [lax.all_gather(one[0], 'dp', axis=1, tiled=True) for one in new]]
    psum x1 -> x0, blocking collectives: 177 us -> none  [step(): squares = lax.psum(sum((jnp.sum(g * g) for g in gradients)), 'dp')]
    pallas_call x0 -> x2, Pallas kernels: none -> 153 us  [call(): pl.pallas_call(lambda *refs: kernel(names, *refs), out_shape=list(outs.va...]
    unnamed x27 -> x0, local copies, waits for them, and re-layouts: 78 us -> none
  transfers between devices with their start and end apart: 4 -> 0, of which waited for: 4 -> 0; matrix products, arithmetic and copies ran while one was open for 2% -> 0% of each run, Pallas kernels for 0% -> 0%
where the time goes in v1:
time: 154 us
  Pallas kernels  153 us (99%)
    pallas_call x2, Pallas kernels, call(): pl.pallas_call(lambda *refs: kernel(names, *refs), out_shape=list(outs.va...  153 us

profile of v1, /device:TPU:0, one launch (start us, length us, event | category | flops | bytes accessed | tf_op | source)
XLA Modules:
  0.0 153.5 jit_solution(10133990281828249999)
XLA Ops:
  0.6 146.5 %main.1 = (bf16[4,4,2,48,1792]{4,3,2,1,0:T(8,128)(2,1)S(1)}, bf16[4,4,2,112,768]{4,3,2,1,0:T(8,128)(2,1)S(1)}, bf16[4,4,4,48,896]{4,3,2,1,0:T(8,128)(2,1)S(1)}, ...) custom-call(bf16[2,4,4,48,1792]{4,3,2,1,0:T(8,128)(2,1)} %bitcast.21, ...), custom_call_target="tpu_custom_call" | custom-call | tf_op jit(solution)/shard_map/main/pallas_call | solution.py:494
  147.2 6.3 %write_kernel.1 = (bf16[2,4,4,48,1792]{4,3,2,1,0:T(8,128)(2,1)}, bf16[2,4,4,112,768]{4,3,2,1,0:T(8,128)(2,1)}, bf16[2,4,4,48,1792]{4,3,2,1,0:T(8,128)(2,1)}, f32...) custom-call(bf16[4,4,2,48,1792]{4,3,2,1,0:T(8,128)(2,1)S(1)} %get-tu, ...), custom_call_target="tpu_custom_call" | custom-call | tf_op jit(solution)/shard_map/write_kernel/pallas_call | solution.py:494

commit v2 on v1

--- a/solution.py
+++ b/solution.py
@@ -40,8 +40,8 @@
         R[n] for n in ("pb", "bs", "qb", "bt", "rb", "fa", "sa", "ra", "fc", "sc", "rc", "tsc", "tc", "ub", "uc", "vc", "nsend", "nrecv")
     )
     ua = sa
-    sent, local, rec1, rec2, rec2b, rec3, recn, rech, recy, reco = (
-        R[n] for n in ("sent", "local", "rec1", "rec2", "rec2b", "rec3", "recn", "rech", "recy", "reco")
+    sent, local, rec1, rec2, rec2b, rec3, recn, rech = (
+        R[n] for n in ("sent", "local", "rec1", "rec2", "rec2b", "rec3", "recn", "rech")
     )
     tokens = iter(range(sent.shape[0]))
     leaving = []
@@ -102,7 +102,7 @@
 
     barrier = pltpu.get_barrier_semaphore()
     for axis in STRIDE:
-        for off in FAR_FIRST:
+        for off in NEAR:
             pl.semaphore_signal(barrier, inc=1, device_id={"dp": to(axis, off)}, device_id_type=pl.DeviceIdType.MESH)
 
     for which, buf in enumerate((own1, own2)):
@@ -111,7 +111,7 @@
             for k in QUARTERS:
                 src = term(w, h, q, at(CHUNK_AXIS[w], offs(w, h)[k]))
                 pltpu.make_async_copy(src, buf[w].at[h, k], local.at[which, w, h]).start()
-    pl.semaphore_wait(barrier, len(STRIDE) * len(FAR_FIRST))
+    pl.semaphore_wait(barrier, len(STRIDE) * len(NEAR))
 
     left1 = [group(r[w]) for w in WEIGHTS]
 
@@ -212,22 +212,22 @@
                 tiles(own2[w].shape[2], put)
                 phase2(k, w, h, -s if k else s)
 
-    for w, h in ALL:
-        s = way(h)
-        if w == DOWN:
-            for k in QUARTERS:
-                cut_down(h, k)
-                wait(qb.at[h, k, 0], rec2b.at[h, k, 0])
-                bs[h, k, 2] = (pieces[w][at("z", s)] + qb[h, k, 0].astype(F32)).astype(BF)
-                phase2b(2, h, k, s)
-        else:
+    for w in qa:
+        for h in FLOWS:
             wait(qa[w].at[h, 0], rec2.at[w // 2, h, 0])
 
             def add2(t, w=w, h=h):
                 own2[w][h, 2, t] = (total(w, h, 2, t) + qa[w][h, 0, t].astype(F32)).astype(BF)
 
             tiles(own2[w].shape[2], add2)
-            phase2(2, w, h, s)
+            phase2(2, w, h, way(h))
+    for k in QUARTERS:
+        for h in FLOWS:
+            s = way(h)
+            cut_down(h, k)
+            wait(qb.at[h, k, 0], rec2b.at[h, k, 0])
+            bs[h, k, 2] = (pieces[DOWN][at("z", s)] + qb[h, k, 0].astype(F32)).astype(BF)
+            phase2b(2, h, k, s)
 
     left_a, left_c, left_b = group(ra), group(rc), group(rb)
     for w in qa:
@@ -328,7 +328,9 @@
     devices = nrecv.shape[0]
     nrecv[me] = nsend[...]
     left = group(nrecv.at[1:devices])
-    fori(devices - 1, lambda i: post(nsend, nrecv.at[me], left, recn.at[0], (me + 1 + i) % devices))
+    away = [(min(i, N - i), i) for i in QUARTERS]
+    for _, i, j, k in sorted((a + b + c, i, j, k) for a, i in away for b, j in away for c, k in away)[:0:-1]:
+        post(nsend, nrecv.at[me], left, recn.at[0], to("x", i) + to("y", j) + to("z", k) - 2 * me)
     for j in FAR_FIRST:
         wait(tc.at[at("z", -j)], rech.at[0, j - 1])
     wait(nrecv.at[1:devices], recn.at[0])
@@ -346,113 +348,142 @@
         step = m * lax.rsqrt(v + 1e-8) + 0.1 * ws[w][h]
         return (ws[w][h] - 0.02 * step).astype(BF)
 
-    def spread_out(i, axis, ref, src, first):
+    def spread_out(i, axis, ref, first):
         left = group(first)
         for j in FAR_FIRST:
-            send(src(at(axis, j)), ref(co[axis]), left, rech.at[i, j - 1], axis, j)
-
-    def arrived(i, axis, ref):
-        for j in FAR_FIRST:
-            wait(ref(at(axis, -j)), rech.at[i, j - 1])
+            send(ref(co[axis]), ref(co[axis]), left, rech.at[i, j], axis, j)
+
+    def arrived(i, axis, ref, j):
+        wait(ref(at(axis, -j)), rech.at[i, j])
 
     for h in BOTH:
         new = adamw(GATE, h)
         vc[2 * h] = new[:, :half]
         vc[2 * h + 1] = new[:, half:]
-    uc[z] = vc[z]
-    spread_out(1, "z", lambda p: uc.at[p], lambda p: vc.at[p], uc.at[0:3])
+    uc[y, z] = vc[z]
+    left = group(uc.at[0:3])
+    left0 = group(uc.at[0, 0:3])
+    for j in (*FAR_FIRST, 0):
+        for i in (*FAR_FIRST, 0):
+            if i or j:
+                src, device = vc.at[at("z", i)], to("y", j) + to("z", i) - me
+                post(src, uc.at[y, z], left if j else left0, rech.at[N, j], device)
     for h in BOTH:
         ua[z, h] = adamw(UP, h)
-    spread_out(2, "z", lambda p: ua.at[p], lambda p: ua.at[z], ua.at[0:3])
+        spread_out(1 + h, "z", lambda p: ua.at[p, h], ua.at[0:3, 0])
     for h in BOTH:
         ub[z, x, h] = adamw(DOWN, h)
-    spread_out(3, "x", lambda p: ub.at[z, p], lambda p: ub.at[z, x], ub.at[0, 0:3])
-
-    def own_out(block, left, recv, axis):
-        for d in BOTH:
-            ref = block(0, None)
-            send(ref, ref, left, recv.at[0, d], axis, way(d))
-
-    def pass_on(block, left, recv, axis):
-        for d in BOTH:
-            wait(block(NEAR[d], None), recv.at[0, d])
-            ref = block(NEAR[d], d)
-            send(ref, ref, left, recv.at[1, d], axis, way(d))
-
-    def passed(block, recv):
-        for d in BOTH:
-            wait(block(2, d), recv.at[1, d])
-
-    def ring(ref, sub):
-        def block(p, d):
-            one = ref(p)
-            return one if d is None else one.at[sub(d)]
-
-        return block
-
-    def one(d):
-        return d
-
-    def two(d):
-        return pl.ds(2 * d, 2)
+    spread_out(3, "x", lambda p: ub.at[z, p], ub.at[0, 0:3])
+
+    class Ring:
+        def __init__(self, ref, sub, left, recv, axis):
+            self.ref, self.sub, self.left, self.recv, self.axis = ref, sub, left, recv, axis
+
+        def half(self, p, h):
+            return self.ref(p).at[self.sub(h)]
+
+        def own(self, h):
+            for d in BOTH:
+                ref = self.half(0, h)
+                send(ref, ref, self.left, self.recv(d, h), self.axis, way(d))
+
+        def owns(self):
+            for h in BOTH:
+                self.own(h)
+
+        def pass_on(self):
+            for d in BOTH:
+                ref = self.half(NEAR[d], d)
+                wait(ref, self.recv(d, d))
+                send(ref, ref, self.left, self.recv(2, d), self.axis, way(d))
+
+        def near(self, d):
+            wait(self.half(NEAR[d], 1 - d), self.recv(d, 1 - d))
+
+        def far(self):
+            for d in BOTH:
+                wait(self.half(2, d), self.recv(2, d))
+
+    def one(h):
+        return h
+
+    def two(h):
+        return pl.ds(2 * h, 2)
+
+    def outer_ring(w, i, left):
+        a, c = AXES[w][0], CHUNK_AXIS[w]
+        return Ring(
+            lambda p: W[w].at[at(a, p), at(c, OUTWARD[i])],
+            two if w == GATE else one,
+            left,
+            lambda u, v: rec1.at[w, u, v, i],
+            a,
+        )
 
     left_o = [group(W[w].at[0:3]) for w in WEIGHTS]
-
-    def outer(w, i):
-        return ring(lambda p: W[w].at[at(AXES[w][0], p), at(CHUNK_AXIS[w], OUTWARD[i])], two if w == GATE else one)
-
-    def outer_start(w, i):
-        own_out(outer(w, i), left_o[w], reco.at[w, i], AXES[w][0])
-
+    outer = [[outer_ring(w, i, left_o[w]) for i in QUARTERS] for w in WEIGHTS]
     left_z, left_y, left_x = group(ub.at[0:3]), group(W[UP].at[0, 0:3]), group(W[GATE].at[0, 0:3])
-    zring = [ring(lambda p, off=off: ub.at[at("z", p), at("x", off)], one) for off in OUTWARD]
-    own_out(zring[0], left_z, recy.at[2], "z")
-
-    arrived(1, "z", lambda p: uc.at[p])
-    W[GATE][z, x, y] = join(GATE, lambda q: uc[q], half)
-    spread_out(4, "y", lambda p: W[GATE].at[z, x, p], lambda p: W[GATE].at[z, x, y], W[GATE].at[0, 0, 0:3])
-
-    arrived(2, "z", lambda p: ua.at[p])
-    for h in BOTH:
-        W[UP][x, y, h] = join(UP, lambda q: ua[q, h], tall[UP].shape[1])
-    yring = ring(lambda p: W[UP].at[x, at("y", p)], one)
-    own_out(yring, left_y, recy.at[0], "y")
-    outer_start(UP, 0)
-
+    zring = [
+        Ring(lambda p, off=off: ub.at[at("z", p), at("x", off)], one, left_z, lambda u, v, i=i: rec2b.at[v, i, u], "z")
+        for i, off in enumerate(OUTWARD)
+    ]
+    yring = Ring(lambda p: W[UP].at[x, at("y", p)], one, left_y, lambda u, v: rec2.at[0, v, u], "y")
+    xring = Ring(lambda p: W[GATE].at[z, at("x", p)], two, left_x, lambda u, v: rec2.at[1, v, u], "x")
+
+    zring[0].owns()
     for i, off in enumerate(OUTWARD):
         if off:
-            wait(ub.at[z, at("x", off)], rech.at[3, -off % N - 1])
-            own_out(zring[i], left_z, recy.at[2 + i], "z")
+            arrived(3, "x", lambda p: ub.at[z, p], -off % N)
+            zring[i].owns()
+    for h in BOTH:
+        for j in FAR_FIRST:
+            arrived(1 + h, "z", lambda p: ua.at[p, h], j)
+        W[UP][x, y, h] = join(UP, lambda q: ua[q, h], tall[UP].shape[1])
+        yring.own(h)
+        outer[UP][0].own(h)
+    zring[0].pass_on()
+    for j in QUARTERS:
+        ref = uc.at[at("y", -j)]
+        wait(ref if j else ref.at[0:3], rech.at[N, j])
+    for b in QUARTERS:
+        W[GATE][z, x, b] = join(GATE, lambda q: uc[b, q], half)
+    xring.owns()
+    outer[GATE][0].owns()
+    zring[1].pass_on()
+    zring[2].pass_on()
+    yring.pass_on()
+    for d in BOTH:
+        yring.near(d)
+        if not d:
+            outer[UP][1].owns()
+    zring[3].pass_on()
+    xring.pass_on()
+    for d in BOTH:
+        xring.near(d)
+        if not d:
+            outer[GATE][1].owns()
     for i in QUARTERS:
-        pass_on(zring[i], left_z, recy.at[2 + i], "z")
-
-    arrived(4, "y", lambda p: W[GATE].at[z, x, p])
-    xring = ring(lambda p: W[GATE].at[z, at("x", p)], two)
-    own_out(xring, left_x, recy.at[1], "x")
-    outer_start(GATE, 0)
-
-    pass_on(yring, left_y, recy.at[0], "y")
-    outer_start(UP, 1)
-    outer_start(UP, 2)
-    for i in QUARTERS:
-        passed(zring[i], recy.at[2 + i])
+        for d in BOTH:
+            zring[i].near(d)
+        zring[i].far()
         c = at("x", OUTWARD[i])
         for h in BOTH:
             W[DOWN][y, c, h] = join(DOWN, lambda q: ub[q, c, h], tall[DOWN].shape[1])
-        outer_start(DOWN, i)
-    pass_on(xring, left_x, recy.at[1], "x")
-    outer_start(GATE, 1)
-    outer_start(GATE, 2)
-    passed(yring, recy.at[0])
-    outer_start(UP, 3)
-    passed(xring, recy.at[1])
-    outer_start(GATE, 3)
+        outer[DOWN][i].owns()
+    outer[UP][2].owns()
+    outer[GATE][2].owns()
+    yring.far()
+    outer[UP][3].owns()
+    xring.far()
+    outer[GATE][3].owns()
     for i in QUARTERS:
         for w in WEIGHTS:
-            pass_on(outer(w, i), left_o[w], reco.at[w, i], AXES[w][0])
+            outer[w][i].pass_on()
     for i in QUARTERS:
         for w in WEIGHTS:
-            passed(outer(w, i), reco.at[w, i])
+            for d in BOTH:
+                outer[w][i].near(d)
+            outer[w][i].far()
     for ref, sem in leaving:
         wait(ref, sem)
 
@@ -551,7 +582,7 @@
             tsc=vm((N, pad, half), BF),
             tc=vm((N, pad, half), BF),
             ub=vm((N, N, 2, pad_d, d), BF),
-            uc=vm((N, pad, half), BF),
+            uc=vm((N, N, pad, half), BF),
             vc=vm((N, pad, half), BF),
             nsend=vm((1, 128), F32),
             nrecv=vm((N**3, 1, 128), F32),
@@ -562,9 +593,7 @@
             rec2b=dma((2, N, 3)),
             rec3=dma((N, 3)),
             recn=dma((1,)),
-            rech=dma((5, 3)),
-            recy=dma((6, 2, 2)),
-            reco=dma((3, N, 2, 2)),
+            rech=dma((N + 1, N)),
         )
         outs = by_weight(
             W=[jax.ShapeDtypeStruct(s, BF) for s in ((N, N, 2, n, ff), (N, N, 2, n_d, d), (N, N, N, n, half))],

time: 154 us -> 156 us (1.013)
  Pallas kernels: 153 us -> 156 us
    pallas_call x2, Pallas kernels: 153 us -> 156 us  [call(): pl.pallas_call(lambda *refs: kernel(names, *refs), out_shape=list(outs.va...]
where the time goes in v2:
time: 156 us
  Pallas kernels  156 us (100%)
    pallas_call x2, Pallas kernels, call(): pl.pallas_call(lambda *refs: kernel(names, *refs), out_shape=list(outs.va...  156 us

profile of v2, /device:TPU:0, one launch (start us, length us, event | category | flops | bytes accessed | tf_op | source)
XLA Modules:
  0.0 156.2 jit_solution(10744923316291427949)
XLA Ops:
  0.6 149.3 %main.1 = (bf16[4,4,2,48,1792]{4,3,2,1,0:T(8,128)(2,1)S(1)}, bf16[4,4,2,112,768]{4,3,2,1,0:T(8,128)(2,1)S(1)}, bf16[4,4,4,48,896]{4,3,2,1,0:T(8,128)(2,1)S(1)}, ...) custom-call(bf16[2,4,4,48,1792]{4,3,2,1,0:T(8,128)(2,1)} %bitcast.21, ...), custom_call_target="tpu_custom_call" | custom-call | tf_op jit(solution)/shard_map/main/pallas_call | solution.py:525
  149.9 6.3 %write_kernel.1 = (bf16[2,4,4,48,1792]{4,3,2,1,0:T(8,128)(2,1)}, bf16[2,4,4,112,768]{4,3,2,1,0:T(8,128)(2,1)}, bf16[2,4,4,48,1792]{4,3,2,1,0:T(8,128)(2,1)}, f32...) custom-call(bf16[4,4,2,48,1792]{4,3,2,1,0:T(8,128)(2,1)S(1)} %get-tu, ...), custom_call_target="tpu_custom_call" | custom-call | tf_op jit(solution)/shard_map/write_kernel/pallas_call | solution.py:525

commit v3 on v2

--- a/solution.py
+++ b/solution.py
@@ -82,22 +82,33 @@
         if w == UP:
             return g[w].at[h, q, c]
         if w == DOWN:
-            return g[w].at[h, c, q]
+            return g[w].at[:, c, q, :, down_cols(h)]
         cols = g[w].shape[-1] // 2
         return g[w].at[q // 2, c, h, :, pl.ds(pl.multiple_of(q % 2 * cols, 128), cols)]
 
-    def tiles(n, body):
-        fori(n // TILE, lambda i: body(pl.ds(pl.multiple_of(i * TILE, TILE), TILE)))
-
-    def cut(w):
-        rows, (_, pad, cols) = vi[w].shape[0], pieces[w].shape
+    def rows_of(i):
+        return pl.ds(pl.multiple_of(i * TILE, TILE), TILE)
+
+    def tiles(w, body):
+        n = own1[w].shape[-2] // TILE
+        if w == DOWN:
+            fori(2 * n, lambda i: body((i // n, rows_of(i % n))))
+        else:
+            fori(n, lambda i: body((rows_of(i),)))
+
+    def down_cols(h):
+        cols = own1[DOWN].shape[-1]
+        return pl.ds(h * cols, cols)
+
+    def cut(w, h):
+        rows, cols = vi[w].shape[0], pieces[w].shape[-1]
         for q in QUARTERS:
-            pieces[w][q] = tall[w][rows * q : rows * q + pad, 0:cols]
-
-    def join(w, piece, cols):
-        rows = vi[w].shape[0]
+            pieces[w][q, rows * h : rows * (h + 1)] = tall[w][rows * q : rows * (q + 1), 0:cols]
+
+    def join(w, h):
+        rows, cols = vi[w].shape[0], pieces[w].shape[-1]
         for q in QUARTERS:
-            tall[w][rows * q : rows * q + rows, 0:cols] = piece(q).astype(F32)[:rows]
+            tall[w][rows * q : rows * (q + 1), 0:cols] = pieces[w][q, rows * h : rows * (h + 1)]
         return tall[w][0 : N * rows, 0:cols].astype(BF)
 
     barrier = pltpu.get_barrier_semaphore()
@@ -140,49 +151,52 @@
             wait(r[w].at[0, h, k], rec1.at[w, 0, h, k])
 
             def add(t, w=w, h=h, k=k):
-                own1[w][h, k, t] = (own1[w][h, k, t].astype(F32) + r[w][0, h, k, t].astype(F32)).astype(BF)
-
-            tiles(own1[w].shape[2], add)
+                t = (h, k, *t)
+                own1[w][t] = (own1[w][t].astype(F32) + r[w][(0, *t)].astype(F32)).astype(BF)
+
+            tiles(w, add)
             phase1(2, w, h, k, own1[w].at[h, k], way(h))
 
+    pieces[GATE][...] = jnp.zeros(pieces[GATE].shape, F32)
     for w in WEIGHTS:
-        rows, (_, pad, cols) = vi[w].shape[0], ms[w].shape
-        if w != GATE:
-            n = N * rows
-            tall[w][n : n + TILE, :] = jnp.zeros((TILE, tall[w].shape[1]), F32)
+        rows = vi[w].shape[0]
         for i, dst in enumerate((wl[w], mv[w].at[0], mv[w].at[1])):
             wait(dst, local.at[2 + i // 2, w, i % 2])
-        for h in BOTH:
-            for dst in (ms[w], vs[w]):
-                dst[h, pad - 8 : pad] = jnp.zeros((8, cols), F32)
-
-        def spread(i, w=w):
+
+        def spread(i, w=w, rows=rows):
             for src, dst in ((mv[w][0, i], ms[w]), (mv[w][1, i], vs[w])):
                 for h in BOTH:
-                    dst[h, pl.ds(i, 1), :] = src[h : h + 1]
+                    dst[pl.ds(rows * h + i, 1), :] = src[h : h + 1]
 
         fori(rows, spread)
-        for h in BOTH:
-
-            def widen(t, w=w, h=h):
-                tall[w][t, :] = wl[w][h, t].astype(F32)
-
-            tiles(N * rows, widen)
-            src = pieces[w] if w != GATE else pieces[UP]
-            cut(w if w != GATE else UP)
-            ws[w][h] = src[z]
+        v = DOWN if w == DOWN else UP
+        for cols in [down_cols(c) for c in BOTH] if w == DOWN else [slice(None)]:
+            for h in BOTH:
+
+                def widen(i, w=w, h=h, v=v, cols=cols):
+                    t = rows_of(i)
+                    tall[v][t, :] = wl[w][h, t, cols].astype(F32)
+
+                fori(N * rows // TILE, widen)
+                cut(v, h)
+            ws[w][:, cols] = pieces[v][z]
         if w == UP:
             load_state(GATE)
 
     def total(w, h, k, t):
-        return own2[w][h, k, t].astype(F32) + r[w][1, h, k, t].astype(F32) + r[w][2, h, k, t].astype(F32)
+        t = (h, k, *t)
+        return own2[w][t].astype(F32) + r[w][(1, *t)].astype(F32) + r[w][(2, *t)].astype(F32)
 
     def cut_down(h, k):
-        def put(t):
-            tall[DOWN][t, :] = total(DOWN, h, k, t)
-
-        tiles(own2[DOWN].shape[2], put)
-        cut(DOWN)
+        n = own2[DOWN].shape[-2]
+        for layer in BOTH:
+
+            def put(i, layer=layer):
+                t = rows_of(i)
+                tall[DOWN][t, :] = total(DOWN, h, k, (layer, t))
+
+            fori(n // TILE, put)
+            cut(DOWN, layer)
 
     left2 = {w: group(qa[w]) for w in qa}
     left2b = group(qb)
@@ -207,9 +221,9 @@
             elif k < 2:
 
                 def put(t, w=w, h=h, k=k):
-                    own2[w][h, k, t] = total(w, h, k, t).astype(BF)
-
-                tiles(own2[w].shape[2], put)
+                    own2[w][(h, k, *t)] = total(w, h, k, t).astype(BF)
+
+                tiles(w, put)
                 phase2(k, w, h, -s if k else s)
 
     for w in qa:
@@ -217,9 +231,9 @@
             wait(qa[w].at[h, 0], rec2.at[w // 2, h, 0])
 
             def add2(t, w=w, h=h):
-                own2[w][h, 2, t] = (total(w, h, 2, t) + qa[w][h, 0, t].astype(F32)).astype(BF)
-
-            tiles(own2[w].shape[2], add2)
+                own2[w][(h, 2, *t)] = (total(w, h, 2, t) + qa[w][(h, 0, *t)].astype(F32)).astype(BF)
+
+            tiles(w, add2)
             phase2(2, w, h, way(h))
     for k in QUARTERS:
         for h in FLOWS:
@@ -236,29 +250,30 @@
                 wait(qa[w].at[h, i], rec2.at[w // 2, h, i])
 
             def total2(t, w=w, h=h):
-                return total(w, h, 3, t) + qa[w][h, 1, t].astype(F32) + qa[w][h, 2, t].astype(F32)
+                return total(w, h, 3, t) + qa[w][(h, 1, *t)].astype(F32) + qa[w][(h, 2, *t)].astype(F32)
 
             if w == UP:
 
                 def put2(t, total2=total2):
-                    tall[UP][t, :] = total2(t)
-
-                tiles(own2[w].shape[2], put2)
-                cut(UP)
-                for q in QUARTERS:
-                    sa[q, h] = pieces[UP][q].astype(BF)
-                fa[h] = pieces[UP][z]
+                    tall[UP][(*t, slice(None))] = total2(t)
+
+                tiles(w, put2)
+                cut(UP, h)
             else:
                 n = fc.shape[1]
                 for b in BOTH:
 
                     def put2(i, total2=total2, h=h, b=b, n=n):
-                        v = total2(pl.ds(pl.multiple_of(b * n + i * TILE, TILE), TILE))
-                        t = pl.ds(pl.multiple_of(i * TILE, TILE), TILE)
+                        v = total2((pl.ds(pl.multiple_of(b * n + i * TILE, TILE), TILE),))
+                        t = rows_of(i)
                         fc[2 * h + b, t] = v
                         sc[2 * h + b, t] = v.astype(BF)
 
                     fori(n // TILE, put2)
+        if w == UP:
+            for q in QUARTERS:
+                sa[q] = pieces[UP][q].astype(BF)
+            fa[...] = pieces[UP][z]
         for j in FAR_FIRST:
             if w == UP:
                 send(sa.at[at("z", j)], ra.at[j - 1], left_a, rec3.at[0, j - 1], "z", j)
@@ -283,9 +298,6 @@
             out = out + v[:, i : i + 128]
         nsend[...] = nsend[...] + out
 
-    def valid(n, v):
-        return jnp.where(lax.broadcasted_iota(jnp.int32, v.shape, 0) < n, v, 0.0)
-
     def rounded(own, others):
         for o in others:
             own = own + o.astype(F32)
@@ -297,13 +309,14 @@
     for j in others:
         wait(rc.at[j], rec3.at[1, j])
 
-    def last_c(t):
+    def last_c(i):
+        t = rows_of(i)
         v = rounded(fc[y, t], [rc[j, t] for j in others])
         tall[UP][t, 0:half] = v
         fold(v)
 
-    tiles(fc.shape[1], last_c)
-    cut(GATE)
+    fori(fc.shape[1] // TILE, last_c)
+    cut(GATE, 0)
     for q in QUARTERS:
         tsc[q] = pieces[GATE][q].astype(BF)
     tc[z] = tsc[z]
@@ -314,16 +327,15 @@
         wait(ra.at[j], rec3.at[0, j])
     (gone,) = [i for i, (_, sem) in enumerate(leaving) if sem is left_a]
     wait(*leaving.pop(gone))
-    for h in BOTH:
-        v = rounded(fa[h], [ra[j, h] for j in others])
-        gf[UP][h] = v
-        fold(valid(vi[UP].shape[0], v))
+    v = rounded(fa[...], [ra[j] for j in others])
+    gf[UP][...] = v
+    fold(v)
     for h in BOTH:
         for k in others:
             wait(rb.at[h, k], rec3.at[2 + h, k])
         v = rounded(pb[h, 3], [rb[h, k] for k in others])
-        gf[DOWN][h] = v
-        fold(valid(vi[DOWN].shape[0], v))
+        gf[DOWN][:, down_cols(h)] = v
+        fold(v)
 
     devices = nrecv.shape[0]
     nrecv[me] = nsend[...]
@@ -336,17 +348,22 @@
     wait(nrecv.at[1:devices], recn.at[0])
     squares = jnp.sum(jnp.sum(nrecv[...], axis=0), axis=1, keepdims=True)
     factor = jnp.minimum(1.0, 0.5 * lax.rsqrt(squares / count + 1e-30))
+    rows = vi[GATE].shape[0]
+
+    def gate_part(q):
+        return slice(rows * (q // 2), rows * (q // 2 + 1)), slice(half * (q % 2), half * (q % 2 + 1))
+
     for q in QUARTERS:
-        gf[GATE][q // 2, :, half * (q % 2) : half * (q % 2 + 1)] = tc[q].astype(F32)
-
-    def adamw(w, h):
-        gc = gf[w][h] * factor
-        m = 0.9 * ms[w][h] + 0.1 * gc
-        v = 0.95 * vs[w][h] + 0.05 * gc * gc
-        mo[w][h] = m
-        vo[w][h] = v
-        step = m * lax.rsqrt(v + 1e-8) + 0.1 * ws[w][h]
-        return (ws[w][h] - 0.02 * step).astype(BF)
+        gf[GATE][gate_part(q)] = tc[q].astype(F32)[:rows]
+
+    def adamw(w):
+        gc = gf[w][...] * factor
+        m = 0.9 * ms[w][...] + 0.1 * gc
+        v = 0.95 * vs[w][...] + 0.05 * gc * gc
+        mo[w][...] = m
+        vo[w][...] = v
+        step = m * lax.rsqrt(v + 1e-8) + 0.1 * ws[w][...]
+        return ws[w][...] - 0.02 * step
 
     def spread_out(i, axis, ref, first):
         left = group(first)
@@ -356,23 +373,17 @@
     def arrived(i, axis, ref, j):
         wait(ref(at(axis, -j)), rech.at[i, j])
 
-    for h in BOTH:
-        new = adamw(GATE, h)
-        vc[2 * h] = new[:, :half]
-        vc[2 * h + 1] = new[:, half:]
-    uc[y, z] = vc[z]
+    pieces[UP][0] = adamw(GATE)
+    for q in QUARTERS:
+        pieces[GATE][q, 0:rows] = pieces[UP][(0, *gate_part(q))]
+        vc[q] = pieces[GATE][q].astype(BF)
+    uc[z] = vc[z]
     left = group(uc.at[0:3])
-    left0 = group(uc.at[0, 0:3])
-    for j in (*FAR_FIRST, 0):
-        for i in (*FAR_FIRST, 0):
-            if i or j:
-                src, device = vc.at[at("z", i)], to("y", j) + to("z", i) - me
-                post(src, uc.at[y, z], left if j else left0, rech.at[N, j], device)
-    for h in BOTH:
-        ua[z, h] = adamw(UP, h)
-        spread_out(1 + h, "z", lambda p: ua.at[p, h], ua.at[0:3, 0])
-    for h in BOTH:
-        ub[z, x, h] = adamw(DOWN, h)
+    for j in FAR_FIRST:
+        send(vc.at[at("z", j)], uc.at[z], left, rech.at[N, j], "z", j)
+    ua[z] = adamw(UP).astype(BF)
+    spread_out(1, "z", lambda p: ua.at[p], ua.at[0:3])
+    ub[z, x] = adamw(DOWN).astype(BF)
     spread_out(3, "x", lambda p: ub.at[z, p], ub.at[0, 0:3])
 
     class Ring:
@@ -424,53 +435,59 @@
     outer = [[outer_ring(w, i, left_o[w]) for i in QUARTERS] for w in WEIGHTS]
     left_z, left_y, left_x = group(ub.at[0:3]), group(W[UP].at[0, 0:3]), group(W[GATE].at[0, 0:3])
     zring = [
-        Ring(lambda p, off=off: ub.at[at("z", p), at("x", off)], one, left_z, lambda u, v, i=i: rec2b.at[v, i, u], "z")
+        Ring(lambda p, off=off: ub.at[at("z", p), at("x", off)], lambda h: (slice(None), down_cols(h)), left_z, lambda u, v, i=i: rec2b.at[v, i, u], "z")
         for i, off in enumerate(OUTWARD)
     ]
     yring = Ring(lambda p: W[UP].at[x, at("y", p)], one, left_y, lambda u, v: rec2.at[0, v, u], "y")
     xring = Ring(lambda p: W[GATE].at[z, at("x", p)], two, left_x, lambda u, v: rec2.at[1, v, u], "x")
 
     zring[0].owns()
+    for j in FAR_FIRST:
+        arrived(N, "z", lambda p: uc.at[p], j)
+    for q in QUARTERS:
+        pieces[GATE][q] = uc[q].astype(F32)
+    W[GATE][z, x, y] = join(GATE, 0)
+    spread_out(N + 1, "y", lambda p: W[GATE].at[z, x, p], W[GATE].at[0, 0, 0:3])
     for i, off in enumerate(OUTWARD):
         if off:
             arrived(3, "x", lambda p: ub.at[z, p], -off % N)
             zring[i].owns()
+    for j in FAR_FIRST:
+        arrived(1, "z", lambda p: ua.at[p], j)
+    for q in QUARTERS:
+        pieces[UP][q] = ua[q].astype(F32)
     for h in BOTH:
-        for j in FAR_FIRST:
-            arrived(1 + h, "z", lambda p: ua.at[p, h], j)
-        W[UP][x, y, h] = join(UP, lambda q: ua[q, h], tall[UP].shape[1])
+        W[UP][x, y, h] = join(UP, h)
         yring.own(h)
         outer[UP][0].own(h)
     zring[0].pass_on()
-    for j in QUARTERS:
-        ref = uc.at[at("y", -j)]
-        wait(ref if j else ref.at[0:3], rech.at[N, j])
-    for b in QUARTERS:
-        W[GATE][z, x, b] = join(GATE, lambda q: uc[b, q], half)
+    for j in FAR_FIRST:
+        arrived(N + 1, "y", lambda p: W[GATE].at[z, x, p], j)
     xring.owns()
+    for i in QUARTERS:
+        if i:
+            zring[i].pass_on()
     outer[GATE][0].owns()
-    zring[1].pass_on()
-    zring[2].pass_on()
     yring.pass_on()
     for d in BOTH:
         yring.near(d)
-        if not d:
-            outer[UP][1].owns()
-    zring[3].pass_on()
-    xring.pass_on()
-    for d in BOTH:
-        xring.near(d)
-        if not d:
-            outer[GATE][1].owns()
+    outer[UP][1].owns()
     for i in QUARTERS:
         for d in BOTH:
             zring[i].near(d)
         zring[i].far()
         c = at("x", OUTWARD[i])
-        for h in BOTH:
-            W[DOWN][y, c, h] = join(DOWN, lambda q: ub[q, c, h], tall[DOWN].shape[1])
+        for d in BOTH:
+            for q in QUARTERS:
+                pieces[DOWN][q] = ub[q, c, :, down_cols(d)].astype(F32)
+            for h in BOTH:
+                W[DOWN][y, c, h, :, down_cols(d)] = join(DOWN, h)
         outer[DOWN][i].owns()
+    xring.pass_on()
+    for d in BOTH:
+        xring.near(d)
     outer[UP][2].owns()
+    outer[GATE][1].owns()
     outer[GATE][2].owns()
     yring.far()
     outer[UP][3].owns()
@@ -507,12 +524,14 @@
         c.start()
     for w in WEIGHTS:
 
-        def gather(i, w=w):
+        rows = R["mb", w].shape[0]
+
+        def gather(i, w=w, rows=rows):
             for n in "mv":
                 for h in BOTH:
-                    R[n + "b", w][i, h : h + 1] = R[n + "o", w][h, pl.ds(i, 1), :]
-
-        fori(R["mb", w].shape[0], gather)
+                    R[n + "b", w][i, h : h + 1] = R[n + "o", w][pl.ds(rows * h + i, 1), :]
+
+        fori(rows, gather)
         for i, n in enumerate("mv"):
             copies.append(pltpu.make_async_copy(R[n + "b", w], R[n + "out", w], R["small"].at[i, w]))
             copies[-1].start()
@@ -550,10 +569,11 @@
         ins = by_weight(g=g, wt=weights, mi=state[0], vi=state[1])
 
         vm, dma = pltpu.VMEM, pltpu.SemaphoreType.DMA
-        pad, pad_d = 16, 32
-        chunk = ((n, ff), (n_d, d), (2 * n, half))
-        own = ((2, pad, ff), (2, pad_d, d), (2, pad, ff))
-        pieces = [vm((N, *s), F32) for s in ((pad, ff), (pad_d, d), (pad, half))]
+        pad = TILE
+        chunk = ((n, ff), (2, n_d, d // 2), (2 * n, half))
+        own = ((2 * rows, ff), (2 * rows_d, d), (2 * rows, ff))
+        down = (2 * rows_d, d // 2)
+        pieces = [vm((N, *s), F32) for s in (own[0], down, (pad, half))]
         scratch = by_weight(
             own1=[vm((2, N, *c), BF) for c in chunk],
             own2=[vm((2, N, *c), BF) for c in chunk],
@@ -562,27 +582,27 @@
             ms=[vm(s, F32) for s in own],
             vs=[vm(s, F32) for s in own],
             pieces=pieces,
-            wl=[vm((2, *c), BF) for c in chunk[:2]],
+            wl=[vm((2, n, ff), BF), vm((2, n_d, d), BF)],
             mv=[vm((2, *a.shape), F32) for a in state[0][:2]],
-            tall=[vm((n + TILE, ff), F32), vm((n_d + TILE, d), F32)],
+            tall=[vm((n, ff), F32), vm((n_d, d // 2), F32)],
         )
         scratch |= {("qa", w): vm((2, 3, *chunk[w]), BF) for w in (UP, GATE)}
         scratch |= dict(
-            pb=vm((2, N, pad_d, d), F32),
-            bs=vm((2, N, 3, pad_d, d), BF),
-            qb=vm((2, N, 3, pad_d, d), BF),
-            bt=vm((2, 3, pad_d, d), BF),
-            rb=vm((2, 3, pad_d, d), BF),
-            fa=vm((2, pad, ff), F32),
-            sa=vm((N, 2, pad, ff), BF),
-            ra=vm((3, 2, pad, ff), BF),
+            pb=vm((2, N, *down), F32),
+            bs=vm((2, N, 3, *down), BF),
+            qb=vm((2, N, 3, *down), BF),
+            bt=vm((2, 3, *down), BF),
+            rb=vm((2, 3, *down), BF),
+            fa=vm(own[0], F32),
+            sa=vm((N, *own[0]), BF),
+            ra=vm((3, *own[0]), BF),
             fc=vm((N, n, half), F32),
             sc=vm((N, n, half), BF),
             rc=vm((3, n, half), BF),
             tsc=vm((N, pad, half), BF),
             tc=vm((N, pad, half), BF),
-            ub=vm((N, N, 2, pad_d, d), BF),
-            uc=vm((N, N, pad, half), BF),
+            ub=vm((N, N, *own[1]), BF),
+            uc=vm((N, pad, half), BF),
             vc=vm((N, pad, half), BF),
             nsend=vm((1, 128), F32),
             nrecv=vm((N**3, 1, 128), F32),
@@ -593,7 +613,7 @@
             rec2b=dma((2, N, 3)),
             rec3=dma((N, 3)),
             recn=dma((1,)),
-            rech=dma((N + 1, N)),
+            rech=dma((N + 2, N)),
         )
         outs = by_weight(
             W=[jax.ShapeDtypeStruct(s, BF) for s in ((N, N, 2, n, ff), (N, N, 2, n_d, d), (N, N, N, n, half))],

time: 156 us -> 147 us (0.942)
  Pallas kernels: 156 us -> 147 us
    pallas_call x2, Pallas kernels: 156 us -> 147 us  [call(): pl.pallas_call(lambda *refs: kernel(names, *refs), out_shape=list(outs.va...]
where the time goes in v3:
time: 147 us
  Pallas kernels  147 us (100%)
    pallas_call x2, Pallas kernels, call(): pl.pallas_call(lambda *refs: kernel(names, *refs), out_shape=list(outs.va...  147 us

profile of v3, /device:TPU:0, one launch (start us, length us, event | category | flops | bytes accessed | tf_op | source)
XLA Modules:
  0.0 147.2 jit_solution(4403659704618119105)
XLA Ops:
  0.6 140.3 %main.1 = (bf16[4,4,2,48,1792]{4,3,2,1,0:T(8,128)(2,1)S(1)}, bf16[4,4,2,112,768]{4,3,2,1,0:T(8,128)(2,1)S(1)}, bf16[4,4,4,48,896]{4,3,2,1,0:T(8,128)(2,1)S(1)}, ...) custom-call(bf16[2,4,4,48,1792]{4,3,2,1,0:T(8,128)(2,1)} %bitcast.21, ...), custom_call_target="tpu_custom_call" | custom-call | tf_op jit(solution)/shard_map/main/pallas_call | solution.py:544
  140.9 6.3 %write_kernel.1 = (bf16[2,4,4,48,1792]{4,3,2,1,0:T(8,128)(2,1)}, bf16[2,4,4,112,768]{4,3,2,1,0:T(8,128)(2,1)}, bf16[2,4,4,48,1792]{4,3,2,1,0:T(8,128)(2,1)}, f32...) custom-call(bf16[4,4,2,48,1792]{4,3,2,1,0:T(8,128)(2,1)S(1)} %get-tu, ...), custom_call_target="tpu_custom_call" | custom-call | tf_op jit(solution)/shard_map/write_kernel/pallas_call | solution.py:544

commit v4 on v3

--- a/solution.py
+++ b/solution.py
@@ -40,8 +40,8 @@
         R[n] for n in ("pb", "bs", "qb", "bt", "rb", "fa", "sa", "ra", "fc", "sc", "rc", "tsc", "tc", "ub", "uc", "vc", "nsend", "nrecv")
     )
     ua = sa
-    sent, local, rec1, rec2, rec2b, rec3, recn, rech = (
-        R[n] for n in ("sent", "local", "rec1", "rec2", "rec2b", "rec3", "recn", "rech")
+    sent, local, rec1, recd, rec2, rec2b, rec3, recn, rech = (
+        R[n] for n in ("sent", "local", "rec1", "recd", "rec2", "rec2b", "rec3", "recn", "rech")
     )
     tokens = iter(range(sent.shape[0]))
     leaving = []
@@ -96,14 +96,19 @@
         else:
             fori(n, lambda i: body((rows_of(i),)))
 
+    def parts(w):
+        cols = own1[w].shape[-1]
+        cut_at = (cols // 128 + 1) // 2 * 128
+        return slice(0, cut_at), slice(cut_at, cols)
+
     def down_cols(h):
         cols = own1[DOWN].shape[-1]
         return pl.ds(h * cols, cols)
 
-    def cut(w, h):
+    def cut(w, h, part=slice(None)):
         rows, cols = vi[w].shape[0], pieces[w].shape[-1]
         for q in QUARTERS:
-            pieces[w][q, rows * h : rows * (h + 1)] = tall[w][rows * q : rows * (q + 1), 0:cols]
+            pieces[w][q, rows * h : rows * (h + 1), part] = tall[w][rows * q : rows * (q + 1), 0:cols][:, part]
 
     def join(w, h):
         rows, cols = vi[w].shape[0], pieces[w].shape[-1]
@@ -116,35 +121,47 @@
         for off in NEAR:
             pl.semaphore_signal(barrier, inc=1, device_id={"dp": to(axis, off)}, device_id_type=pl.DeviceIdType.MESH)
 
+    early = three("early")
+
+    def first_term(w, h):
+        return term(w, h, at(AXES[w][0], 2), at(CHUNK_AXIS[w], offs(w, h)[0]))
+
+    for w, h in ALL:
+        pltpu.make_async_copy(first_term(w, h), early[w].at[h], local.at[5, w]).start()
     for which, buf in enumerate((own1, own2)):
         for w, h in ALL:
             q = at(AXES[w][0], way(h) * (1 - which))
             for k in QUARTERS:
                 src = term(w, h, q, at(CHUNK_AXIS[w], offs(w, h)[k]))
-                pltpu.make_async_copy(src, buf[w].at[h, k], local.at[which, w, h]).start()
+                pltpu.make_async_copy(src, buf[w].at[h, k], local.at[which, w]).start()
     pl.semaphore_wait(barrier, len(STRIDE) * len(NEAR))
 
+    for w in WEIGHTS:
+        wait(early[w], local.at[5, w])
     left1 = [group(r[w]) for w in WEIGHTS]
 
     def phase1(i, w, h, k, src, off):
-        send(src, r[w].at[i, h, k], left1[w], rec1.at[w, i, h, k], AXES[w][0], off)
+        sem = recd.at[w, h] if i == 1 else rec1.at[w, i // 2, h, k]
+        send(src, r[w].at[i, h, k], left1[w], sem, AXES[w][0], off)
 
     for i, (far, near) in enumerate(((2, 1), (-1, -1))):
         for k in QUARTERS:
             for w, h in ALL:
                 s = way(h)
-                src = term(w, h, at(AXES[w][0], far * s), at(CHUNK_AXIS[w], offs(w, h)[k]))
+                src = early[w].at[h]
+                if i or k:
+                    src = term(w, h, at(AXES[w][0], far * s), at(CHUNK_AXIS[w], offs(w, h)[k]))
                 phase1(i, w, h, k, src, near * s)
 
     def load_state(w):
         for i, (src, dst) in enumerate(((wt[w].at[:, x, y], wl[w]), (mi[w], mv[w].at[0]), (vi[w], mv[w].at[1]))):
-            pltpu.make_async_copy(src, dst, local.at[2 + i // 2, w, i % 2]).start()
+            pltpu.make_async_copy(src, dst, local.at[2 + i, w]).start()
 
     load_state(UP)
     load_state(DOWN)
     for which, buf in enumerate((own1, own2)):
-        for w, h in ALL:
-            wait(buf[w].at[h], local.at[which, w, h])
+        for w in WEIGHTS:
+            wait(buf[w], local.at[which, w])
 
     for k in QUARTERS:
         for w, h in ALL:
@@ -161,7 +178,7 @@
     for w in WEIGHTS:
         rows = vi[w].shape[0]
         for i, dst in enumerate((wl[w], mv[w].at[0], mv[w].at[1])):
-            wait(dst, local.at[2 + i // 2, w, i % 2])
+            wait(dst, local.at[2 + i, w])
 
         def spread(i, w=w, rows=rows):
             for src, dst in ((mv[w][0, i], ms[w]), (mv[w][1, i], vs[w])):
@@ -201,17 +218,21 @@
     left2 = {w: group(qa[w]) for w in qa}
     left2b = group(qb)
 
-    def phase2(i, w, h, off):
-        send(own2[w].at[h, i], qa[w].at[h, i], left2[w], rec2.at[w // 2, h, i], AXES[w][1], off)
+    def phase2(i, w, h, off, part=None):
+        for p in BOTH if part is None else (part,):
+            cols = (slice(None), parts(w)[p])
+            src, dst = own2[w].at[h, i], qa[w].at[h, i]
+            send(src.at[cols], dst.at[cols], left2[w], rec2.at[w // 2, h, p, min(i, 1)], AXES[w][1], off)
 
     def phase2b(i, h, k, off):
-        send(bs.at[h, k, i], qb.at[h, k, i], left2b, rec2b.at[h, k, i], "z", off)
+        send(bs.at[h, k, i], qb.at[h, k, i], left2b, rec2b.at[h, k, min(i, 1)], "z", off)
 
     for k in QUARTERS:
         for w, h in ALL:
             s = way(h)
-            for i in (1, 2):
-                wait(r[w].at[i, h, k], rec1.at[w, i, h, k])
+            if not k:
+                wait(r[w].at[1, h], recd.at[w, h])
+            wait(r[w].at[2, h, k], rec1.at[w, 1, h, k])
             if w == DOWN:
                 cut_down(h, k)
                 pb[h, k] = pieces[w][z]
@@ -226,16 +247,20 @@
                 tiles(w, put)
                 phase2(k, w, h, -s if k else s)
 
-    for w in qa:
-        for h in FLOWS:
-            wait(qa[w].at[h, 0], rec2.at[w // 2, h, 0])
-
-            def add2(t, w=w, h=h):
-                own2[w][(h, 2, *t)] = (total(w, h, 2, t) + qa[w][(h, 0, *t)].astype(F32)).astype(BF)
-
-            tiles(w, add2)
-            phase2(2, w, h, way(h))
-    for k in QUARTERS:
+    def running(p):
+        for w in qa:
+            cols = parts(w)[p]
+            for h in FLOWS:
+                wait(qa[w].at[h, 0, :, cols], rec2.at[w // 2, h, p, 0])
+
+                def add2(t, w=w, h=h, cols=cols):
+                    t = (*t, cols)
+                    own2[w][(h, 2, *t)] = (total(w, h, 2, t) + qa[w][(h, 0, *t)].astype(F32)).astype(BF)
+
+                tiles(w, add2)
+                phase2(2, w, h, way(h), p)
+
+    def running_down(k):
         for h in FLOWS:
             s = way(h)
             cut_down(h, k)
@@ -244,52 +269,67 @@
             phase2b(2, h, k, s)
 
     left_a, left_c, left_b = group(ra), group(rc), group(rb)
-    for w in qa:
+
+    def last_sends(p):
+        for w in qa:
+            cols = parts(w)[p]
+            for h in BOTH:
+                wait(qa[w].at[h, 1:3, :, cols], rec2.at[w // 2, h, p, 1])
+
+                def total2(t, w=w, h=h, cols=cols):
+                    t = (*t, cols)
+                    return total(w, h, 3, t) + qa[w][(h, 1, *t)].astype(F32) + qa[w][(h, 2, *t)].astype(F32)
+
+                if w == UP:
+
+                    def put2(t, total2=total2, cols=cols):
+                        tall[UP][(*t, cols)] = total2(t)
+
+                    tiles(w, put2)
+                    cut(UP, h, cols)
+                else:
+                    n = fc.shape[1]
+                    for b in BOTH:
+
+                        def put2(i, total2=total2, h=h, b=b, n=n, cols=cols):
+                            v = total2((pl.ds(pl.multiple_of(b * n + i * TILE, TILE), TILE),))
+                            t = rows_of(i)
+                            fc[2 * h + b, t, cols] = v
+                            sc[2 * h + b, t, cols] = v.astype(BF)
+
+                        fori(n // TILE, put2)
+            if w == UP:
+                for q in QUARTERS:
+                    sa[q, :, cols] = pieces[UP][q, :, cols].astype(BF)
+                fa[:, cols] = pieces[UP][z, :, cols]
+            for j in FAR_FIRST:
+                src, dst, left, axis = (sa, ra, left_a, "z") if w == UP else (sc, rc, left_c, "y")
+                send(src.at[at(axis, j), :, cols], dst.at[j - 1, :, cols], left, rec3.at[w // 2, p], axis, j)
+
+    def last_sends_down(k):
         for h in BOTH:
-            for i in (1, 2):
-                wait(qa[w].at[h, i], rec2.at[w // 2, h, i])
-
-            def total2(t, w=w, h=h):
-                return total(w, h, 3, t) + qa[w][(h, 1, *t)].astype(F32) + qa[w][(h, 2, *t)].astype(F32)
-
-            if w == UP:
-
-                def put2(t, total2=total2):
-                    tall[UP][(*t, slice(None))] = total2(t)
-
-                tiles(w, put2)
-                cut(UP, h)
-            else:
-                n = fc.shape[1]
-                for b in BOTH:
-
-                    def put2(i, total2=total2, h=h, b=b, n=n):
-                        v = total2((pl.ds(pl.multiple_of(b * n + i * TILE, TILE), TILE),))
-                        t = rows_of(i)
-                        fc[2 * h + b, t] = v
-                        sc[2 * h + b, t] = v.astype(BF)
-
-                    fori(n // TILE, put2)
-        if w == UP:
-            for q in QUARTERS:
-                sa[q] = pieces[UP][q].astype(BF)
-            fa[...] = pieces[UP][z]
-        for j in FAR_FIRST:
-            if w == UP:
-                send(sa.at[at("z", j)], ra.at[j - 1], left_a, rec3.at[0, j - 1], "z", j)
-            else:
-                send(sc.at[at("y", j)], rc.at[j - 1], left_c, rec3.at[1, j - 1], "y", j)
-    for k in QUARTERS:
-        for h in BOTH:
-            for i in (1, 2):
-                wait(qb.at[h, k, i], rec2b.at[h, k, i])
+            wait(qb.at[h, k, 1:3], rec2b.at[h, k, 1])
             v = pb[h, k] + qb[h, k, 1].astype(F32) + qb[h, k, 2].astype(F32)
             off = offs(DOWN, h)[k]
             if off:
                 bt[h, k] = v.astype(BF)
-                send(bt.at[h, k], rb.at[h, k], left_b, rec3.at[2 + h, k], "x", off)
+                send(bt.at[h, k], rb.at[h, k], left_b, rec3.at[2, h], "x", off)
             else:
                 pb[h, k] = v
+
+    first, second = BOTH
+    running(first)
+    running_down(0)
+    running_down(1)
+    running(second)
+    running_down(2)
+    running_down(3)
+    last_sends(first)
+    last_sends_down(0)
+    last_sends_down(1)
+    last_sends(second)
+    last_sends_down(2)
+    last_sends_down(3)
 
     def fold(v):
         v = jnp.sum(v * v, axis=0, keepdims=True)
@@ -306,8 +346,8 @@
     others = range(len(FAR_FIRST))
     half = tsc.shape[-1]
     nsend[...] = jnp.zeros(nsend.shape, F32)
-    for j in others:
-        wait(rc.at[j], rec3.at[1, j])
+    for p in BOTH:
+        wait(rc.at[:, :, parts(GATE)[p]], rec3.at[1, p])
 
     def last_c(i):
         t = rows_of(i)
@@ -322,17 +362,16 @@
     tc[z] = tsc[z]
     left = group(tc.at[0:3])
     for j in FAR_FIRST:
-        send(tsc.at[at("z", j)], tc.at[z], left, rech.at[0, j - 1], "z", j)
-    for j in others:
-        wait(ra.at[j], rec3.at[0, j])
+        send(tsc.at[at("z", j)], tc.at[z], left, rech.at[0], "z", j)
+    for p in BOTH:
+        wait(ra.at[:, :, parts(UP)[p]], rec3.at[0, p])
     (gone,) = [i for i, (_, sem) in enumerate(leaving) if sem is left_a]
     wait(*leaving.pop(gone))
     v = rounded(fa[...], [ra[j] for j in others])
     gf[UP][...] = v
     fold(v)
     for h in BOTH:
-        for k in others:
-            wait(rb.at[h, k], rec3.at[2 + h, k])
+        wait(rb.at[h], rec3.at[2, h])
         v = rounded(pb[h, 3], [rb[h, k] for k in others])
         gf[DOWN][:, down_cols(h)] = v
         fold(v)
@@ -343,8 +382,7 @@
     away = [(min(i, N - i), i) for i in QUARTERS]
     for _, i, j, k in sorted((a + b + c, i, j, k) for a, i in away for b, j in away for c, k in away)[:0:-1]:
         post(nsend, nrecv.at[me], left, recn.at[0], to("x", i) + to("y", j) + to("z", k) - 2 * me)
-    for j in FAR_FIRST:
-        wait(tc.at[at("z", -j)], rech.at[0, j - 1])
+    wait(tc.at[0:3], rech.at[0])
     wait(nrecv.at[1:devices], recn.at[0])
     squares = jnp.sum(jnp.sum(nrecv[...], axis=0), axis=1, keepdims=True)
     factor = jnp.minimum(1.0, 0.5 * lax.rsqrt(squares / count + 1e-30))
@@ -368,10 +406,7 @@
     def spread_out(i, axis, ref, first):
         left = group(first)
         for j in FAR_FIRST:
-            send(ref(co[axis]), ref(co[axis]), left, rech.at[i, j], axis, j)
-
-    def arrived(i, axis, ref, j):
-        wait(ref(at(axis, -j)), rech.at[i, j])
+            send(ref(co[axis]), ref(co[axis]), left, rech.at[i], axis, j)
 
     pieces[UP][0] = adamw(GATE)
     for q in QUARTERS:
@@ -380,11 +415,13 @@
     uc[z] = vc[z]
     left = group(uc.at[0:3])
     for j in FAR_FIRST:
-        send(vc.at[at("z", j)], uc.at[z], left, rech.at[N, j], "z", j)
+        send(vc.at[at("z", j)], uc.at[z], left, rech.at[2], "z", j)
     ua[z] = adamw(UP).astype(BF)
     spread_out(1, "z", lambda p: ua.at[p], ua.at[0:3])
     ub[z, x] = adamw(DOWN).astype(BF)
-    spread_out(3, "x", lambda p: ub.at[z, p], ub.at[0, 0:3])
+    left = group(ub.at[0, 0:3])
+    for j in FAR_FIRST:
+        send(ub.at[z, x], ub.at[z, x], left, rech.at[N + j], "x", j)
 
     class Ring:
         def __init__(self, ref, sub, left, recv, axis):
@@ -427,7 +464,7 @@
             lambda p: W[w].at[at(a, p), at(c, OUTWARD[i])],
             two if w == GATE else one,
             left,
-            lambda u, v: rec1.at[w, u, v, i],
+            lambda u, v: rec1.at[w, 0, u, i] if u == v else recd.at[w, u // 2],
             a,
         )
 
@@ -435,25 +472,23 @@
     outer = [[outer_ring(w, i, left_o[w]) for i in QUARTERS] for w in WEIGHTS]
     left_z, left_y, left_x = group(ub.at[0:3]), group(W[UP].at[0, 0:3]), group(W[GATE].at[0, 0:3])
     zring = [
-        Ring(lambda p, off=off: ub.at[at("z", p), at("x", off)], lambda h: (slice(None), down_cols(h)), left_z, lambda u, v, i=i: rec2b.at[v, i, u], "z")
+        Ring(lambda p, off=off: ub.at[at("z", p), at("x", off)], lambda h: (slice(None), down_cols(h)), left_z, lambda u, v, i=i: rec2b.at[u, i, 0] if u == v else rec2b.at[0, i, 1], "z")
         for i, off in enumerate(OUTWARD)
     ]
-    yring = Ring(lambda p: W[UP].at[x, at("y", p)], one, left_y, lambda u, v: rec2.at[0, v, u], "y")
-    xring = Ring(lambda p: W[GATE].at[z, at("x", p)], two, left_x, lambda u, v: rec2.at[1, v, u], "x")
+    yring = Ring(lambda p: W[UP].at[x, at("y", p)], one, left_y, lambda u, v: rec2.at[0, v, u % 2, u // 2], "y")
+    xring = Ring(lambda p: W[GATE].at[z, at("x", p)], two, left_x, lambda u, v: rec2.at[1, v, u % 2, u // 2], "x")
 
     zring[0].owns()
-    for j in FAR_FIRST:
-        arrived(N, "z", lambda p: uc.at[p], j)
+    wait(uc.at[0:3], rech.at[2])
     for q in QUARTERS:
         pieces[GATE][q] = uc[q].astype(F32)
     W[GATE][z, x, y] = join(GATE, 0)
-    spread_out(N + 1, "y", lambda p: W[GATE].at[z, x, p], W[GATE].at[0, 0, 0:3])
+    spread_out(3, "y", lambda p: W[GATE].at[z, x, p], W[GATE].at[0, 0, 0:3])
     for i, off in enumerate(OUTWARD):
         if off:
-            arrived(3, "x", lambda p: ub.at[z, p], -off % N)
+            wait(ub.at[z, at("x", off)], rech.at[N - off % N + N])
             zring[i].owns()
-    for j in FAR_FIRST:
-        arrived(1, "z", lambda p: ua.at[p], j)
+    wait(ua.at[0:3], rech.at[1])
     for q in QUARTERS:
         pieces[UP][q] = ua[q].astype(F32)
     for h in BOTH:
@@ -461,8 +496,7 @@
         yring.own(h)
         outer[UP][0].own(h)
     zring[0].pass_on()
-    for j in FAR_FIRST:
-        arrived(N + 1, "y", lambda p: W[GATE].at[z, x, p], j)
+    wait(W[GATE].at[0, 0, 0:3], rech.at[3])
     xring.owns()
     for i in QUARTERS:
         if i:
@@ -473,9 +507,7 @@
         yring.near(d)
     outer[UP][1].owns()
     for i in QUARTERS:
-        for d in BOTH:
-            zring[i].near(d)
-        zring[i].far()
+        wait(ub.at[0:2, 0], rec2b.at[0, i, 1])
         c = at("x", OUTWARD[i])
         for d in BOTH:
             for q in QUARTERS:
@@ -496,11 +528,9 @@
     for i in QUARTERS:
         for w in WEIGHTS:
             outer[w][i].pass_on()
-    for i in QUARTERS:
-        for w in WEIGHTS:
-            for d in BOTH:
-                outer[w][i].near(d)
-            outer[w][i].far()
+    for w in WEIGHTS:
+        for i in BOTH:
+            wait(W[w].at[0], recd.at[w, i])
     for ref, sem in leaving:
         wait(ref, sem)
 
@@ -577,6 +607,7 @@
         scratch = by_weight(
             own1=[vm((2, N, *c), BF) for c in chunk],
             own2=[vm((2, N, *c), BF) for c in chunk],
+            early=[vm((2, *c), BF) for c in chunk],
             r=[vm((3, 2, N, *c), BF) for c in chunk],
             ws=[vm(s, F32) for s in own],
             ms=[vm(s, F32) for s in own],
@@ -607,13 +638,14 @@
             nsend=vm((1, 128), F32),
             nrecv=vm((N**3, 1, 128), F32),
             sent=dma((24,)),
-            local=dma((N, 3, 2)),
-            rec1=dma((3, 3, 2, N)),
-            rec2=dma((2, 2, 3)),
-            rec2b=dma((2, N, 3)),
-            rec3=dma((N, 3)),
+            local=dma((6, 3)),
+            rec1=dma((3, 2, 2, N)),
+            recd=dma((3, 2)),
+            rec2=dma((2, 2, 2, 2)),
+            rec2b=dma((2, N, 2)),
+            rec3=dma((3, 2)),
             recn=dma((1,)),
-            rech=dma((N + 2, N)),
+            rech=dma((2 * N,)),
         )
         outs = by_weight(
             W=[jax.ShapeDtypeStruct(s, BF) for s in ((N, N, 2, n, ff), (N, N, 2, n_d, d), (N, N, N, n, half))],
@@ -625,7 +657,7 @@
         def main(names, *refs):
             main_kernel(names, count, *refs)
 
-        got = call(main, ins, outs, scratch, pltpu.HBM, vm, collective_id=0, has_side_effects=True, vmem_limit_bytes=36900000)
+        got = call(main, ins, outs, scratch, pltpu.HBM, vm, collective_id=0, has_side_effects=True, vmem_limit_bytes=37600000)
         small = [jax.ShapeDtypeStruct(a.shape, F32) for a in state[0]]
         outs = by_weight(out=[jax.ShapeDtypeStruct(s, BF) for s in full], mout=small, vout=small)
         scratch = by_weight(mb=[vm(a.shape, F32) for a in small], vb=[vm(a.shape, F32) for a in small])

time: 147 us -> 146 us (level)
  Pallas kernels: 147 us -> 145 us
where the time goes in v4:
time: 146 us
  Pallas kernels  145 us (99%)
    pallas_call x2, Pallas kernels, call(): pl.pallas_call(lambda *refs: kernel(names, *refs), out_shape=list(outs.va...  145 us

profile of v4, /device:TPU:0, one launch (start us, length us, event | category | flops | bytes accessed | tf_op | source)
XLA Modules:
  0.0 145.9 jit_solution(7484093682349055756)
XLA Ops:
  0.6 139.0 %main.1 = (bf16[4,4,2,48,1792]{4,3,2,1,0:T(8,128)(2,1)S(1)}, bf16[4,4,2,112,768]{4,3,2,1,0:T(8,128)(2,1)S(1)}, bf16[4,4,4,48,896]{4,3,2,1,0:T(8,128)(2,1)S(1)}, ...) custom-call(bf16[2,4,4,48,1792]{4,3,2,1,0:T(8,128)(2,1)} %bitcast.21, ...), custom_call_target="tpu_custom_call" | custom-call | tf_op jit(solution)/shard_map/main/pallas_call | solution.py:574
  139.6 6.3 %write_kernel.1 = (bf16[2,4,4,48,1792]{4,3,2,1,0:T(8,128)(2,1)}, bf16[2,4,4,112,768]{4,3,2,1,0:T(8,128)(2,1)}, bf16[2,4,4,48,1792]{4,3,2,1,0:T(8,128)(2,1)}, f32...) custom-call(bf16[4,4,2,48,1792]{4,3,2,1,0:T(8,128)(2,1)S(1)} %get-tu, ...), custom_call_target="tpu_custom_call" | custom-call | tf_op jit(solution)/shard_map/write_kernel/pallas_call | solution.py:574

commit v5 on v4

--- a/solution.py
+++ b/solution.py
@@ -98,7 +98,7 @@
 
     def parts(w):
         cols = own1[w].shape[-1]
-        cut_at = (cols // 128 + 1) // 2 * 128
+        cut_at = (cols // 128 * 2 + 1) // 3 * 128
         return slice(0, cut_at), slice(cut_at, cols)
 
     def down_cols(h):

time: 146 us -> 145 us (level)
  no operation moved by 1% of the time
where the time goes in v5:
time: 145 us
  Pallas kernels  144 us (99%)
    pallas_call x2, Pallas kernels, call(): pl.pallas_call(lambda *refs: kernel(names, *refs), out_shape=list(outs.va...  144 us

profile of v5, /device:TPU:0, one launch (start us, length us, event | category | flops | bytes accessed | tf_op | source)
XLA Modules:
  0.0 144.7 jit_solution(11086486538774987594)
XLA Ops:
  0.6 137.8 %main.1 = (bf16[4,4,2,48,1792]{4,3,2,1,0:T(8,128)(2,1)S(1)}, bf16[4,4,2,112,768]{4,3,2,1,0:T(8,128)(2,1)S(1)}, bf16[4,4,4,48,896]{4,3,2,1,0:T(8,128)(2,1)S(1)}, ...) custom-call(bf16[2,4,4,48,1792]{4,3,2,1,0:T(8,128)(2,1)} %bitcast.21, ...), custom_call_target="tpu_custom_call" | custom-call | tf_op jit(solution)/shard_map/main/pallas_call | solution.py:574
  138.4 6.3 %write_kernel.1 = (bf16[2,4,4,48,1792]{4,3,2,1,0:T(8,128)(2,1)}, bf16[2,4,4,112,768]{4,3,2,1,0:T(8,128)(2,1)}, bf16[2,4,4,48,1792]{4,3,2,1,0:T(8,128)(2,1)}, f32...) custom-call(bf16[4,4,2,48,1792]{4,3,2,1,0:T(8,128)(2,1)S(1)} %get-tu, ...), custom_call_target="tpu_custom_call" | custom-call | tf_op jit(solution)/shard_map/write_kernel/pallas_call | solution.py:574

commit v6 on v5

--- a/solution.py
+++ b/solution.py
@@ -127,7 +127,7 @@
         return term(w, h, at(AXES[w][0], 2), at(CHUNK_AXIS[w], offs(w, h)[0]))
 
     for w, h in ALL:
-        pltpu.make_async_copy(first_term(w, h), early[w].at[h], local.at[5, w]).start()
+        pltpu.make_async_copy(first_term(w, h), early[w].at[h], local.at[N, w]).start()
     for which, buf in enumerate((own1, own2)):
         for w, h in ALL:
             q = at(AXES[w][0], way(h) * (1 - which))
@@ -137,7 +137,7 @@
     pl.semaphore_wait(barrier, len(STRIDE) * len(NEAR))
 
     for w in WEIGHTS:
-        wait(early[w], local.at[5, w])
+        wait(early[w], local.at[N, w])
     left1 = [group(r[w]) for w in WEIGHTS]
 
     def phase1(i, w, h, k, src, off):
@@ -155,7 +155,7 @@
 
     def load_state(w):
         for i, (src, dst) in enumerate(((wt[w].at[:, x, y], wl[w]), (mi[w], mv[w].at[0]), (vi[w], mv[w].at[1]))):
-            pltpu.make_async_copy(src, dst, local.at[2 + i, w]).start()
+            pltpu.make_async_copy(src, dst, local.at[2 + min(i, 1), w]).start()
 
     load_state(UP)
     load_state(DOWN)
@@ -177,7 +177,7 @@
     pieces[GATE][...] = jnp.zeros(pieces[GATE].shape, F32)
     for w in WEIGHTS:
         rows = vi[w].shape[0]
-        for i, dst in enumerate((wl[w], mv[w].at[0], mv[w].at[1])):
+        for i, dst in enumerate((wl[w], mv[w])):
             wait(dst, local.at[2 + i, w])
 
         def spread(i, w=w, rows=rows):
@@ -637,8 +637,8 @@
             vc=vm((N, pad, half), BF),
             nsend=vm((1, 128), F32),
             nrecv=vm((N**3, 1, 128), F32),
-            sent=dma((24,)),
-            local=dma((6, 3)),
+            sent=dma((21,)),
+            local=dma((N + 1, 3)),
             rec1=dma((3, 2, 2, N)),
             recd=dma((3, 2)),
             rec2=dma((2, 2, 2, 2)),

time: 145 us -> 145 us (level)
  no operation moved by 1% of the time
where the time goes in v6:
time: 145 us
  Pallas kernels  144 us (99%)
    pallas_call x2, Pallas kernels, call(): pl.pallas_call(lambda *refs: kernel(names, *refs), out_shape=list(outs.va...  144 us

profile of v6, /device:TPU:0, one launch (start us, length us, event | category | flops | bytes accessed | tf_op | source)
XLA Modules:
  0.0 144.7 jit_solution(16127726180524700109)
XLA Ops:
  0.6 137.7 %main.1 = (bf16[4,4,2,48,1792]{4,3,2,1,0:T(8,128)(2,1)S(1)}, bf16[4,4,2,112,768]{4,3,2,1,0:T(8,128)(2,1)S(1)}, bf16[4,4,4,48,896]{4,3,2,1,0:T(8,128)(2,1)S(1)}, ...) custom-call(bf16[2,4,4,48,1792]{4,3,2,1,0:T(8,128)(2,1)} %bitcast.21, ...), custom_call_target="tpu_custom_call" | custom-call | tf_op jit(solution)/shard_map/main/pallas_call | solution.py:574
  138.4 6.3 %write_kernel.1 = (bf16[2,4,4,48,1792]{4,3,2,1,0:T(8,128)(2,1)}, bf16[2,4,4,112,768]{4,3,2,1,0:T(8,128)(2,1)}, bf16[2,4,4,48,1792]{4,3,2,1,0:T(8,128)(2,1)}, f32...) custom-call(bf16[4,4,2,48,1792]{4,3,2,1,0:T(8,128)(2,1)S(1)} %get-tu, ...), custom_call_target="tpu_custom_call" | custom-call | tf_op jit(solution)/shard_map/write_kernel/pallas_call | solution.py:574
